TPU v7x, 32 devices: a 4x4x1 block of a 4x4x8 slice. The times are simulated.
32 devices in a mesh: data: 1 (over z), fsdp: 4 (over y), tp: 8 (over x, core).
Axes of the slice: x: 4, y: 4, z: 1, core: 2. Of those that a mesh axis runs over, the one named last changes fastest.
The devices are a block of a 4x4x8 slice.
Arguments:
- hidden: bfloat16 [8192, 6144], P(('data', 'fsdp', 'tp'))
- ln_scale: float32 [6144], replicated
- w_in: bfloat16 [6144, 24576], P('fsdp', 'tp')
- w_out: bfloat16 [24576, 6144], P(('tp', 'fsdp'))
Outputs:
- output: bfloat16 [8192, 6144], P(('data', 'fsdp', 'tp'))
All inputs are finite; a program needn't handle non-finite values.
Results may differ from a plain program's by a relative error of at most 0.00102.
Values are sent between devices in bfloat16 or wider.
A program may use at most 768 MiB of HBM per device.

v0:
```python
import jax
import jax.numpy as jnp
from jax import lax
from jax.sharding import PartitionSpec as P, NamedSharding

LN_EPS = 1e-6


def layer_norm(row_block, ln_scale):
    block_f32 = row_block.astype(jnp.float32)
    centered = block_f32 - jnp.mean(block_f32, axis=-1, keepdims=True)
    var_row = jnp.mean(centered * centered, axis=-1, keepdims=True)
    return (centered * lax.rsqrt(var_row + LN_EPS) * ln_scale).astype(jnp.bfloat16)


def solution(mesh):
    def local_mlp(hidden, ln_scale, w_in, w_out):
        normed = layer_norm(hidden, ln_scale)
        w_in_tp = lax.all_gather(w_in, "fsdp", axis=0, tiled=True)
        w_out_tp = lax.all_gather(w_out, "fsdp", axis=0, tiled=True)
        group_normed = lax.all_gather(normed, "tp", axis=0, tiled=True)
        pre_act = jnp.dot(group_normed, w_in_tp, preferred_element_type=jnp.float32)
        act_out = jax.nn.gelu(pre_act, approximate=True).astype(jnp.bfloat16)
        part_sum = jnp.dot(act_out, w_out_tp, preferred_element_type=jnp.float32)
        mlp_out = lax.psum_scatter(part_sum, "tp", scatter_dimension=0, tiled=True)
        return (hidden.astype(jnp.float32) + mlp_out).astype(jnp.bfloat16)

    return jax.shard_map(
        local_mlp,
        mesh=mesh,
        in_specs=(P(("data", "fsdp", "tp"), None), P(None), P("fsdp", "tp"), P(("tp", "fsdp"), None)),
        out_specs=P(("data", "fsdp", "tp"), None),
        check_vma=False,
    )
```

profile of v0, /device:TPU:97, one launch (start us, length us, event | category | flops | bytes accessed | tf_op | source)
XLA Modules:
  0.0 1151.7 jit_solution(12358758486873938615)
XLA Ops:
  6.5 0.0 all-gather.4.cloned.1.call-start
  6.6 2.4 convert_reduce_fusion
  9.0 2.9 fusion.16
  11.8 4.8 fusion.18
  16.6 0.1 all-gather.4.cloned.1.call-update
  16.7 0.1 all-gather.6.cloned.1.call-start
  16.8 0.7 all-gather.6.cloned.1.call-update
  17.5 0.1 all-gather.8.cloned.1.call-start
  17.6 0.7 all-gather.8.cloned.1.call-update
  18.3 0.1 reduce-scatter.2.cloned.1.call-start
  18.4 121.1 %all-gather.4.cloned.1.call-done = bf16[2048,6144]{1,0:T(8,128)(2,1)} async-done(((bf16[256,6144]{1,0:T(8,128)(2,1)}), bf16[2048,6144]{1,0:T(8,128)(2,1)}) %all-gather.4.cloned.1.call-update) | async-done | bytes 25165840 | tf_op jit(solution)/shard_map/all_gather | solution.py:21
  139.4 329.1 %all-gather.6.cloned.1.call-done = bf16[6144,3072]{1,0:T(8,128)(2,1)} async-done(((bf16[1536,3072]{1,0:T(8,128)(2,1)}), bf16[6144,3072]{1,0:T(8,128)(2,1)}) %all-gather.6.cloned.1.call-update) | async-done | bytes 37748752 | tf_op jit(solution)/shard_map/all_gather | solution.py:19
  468.6 88.2 %fusion.24 = f32[2048,3072]{1,0:T(8,128)} fusion(bf16[2048,6144]{1,0:T(8,128)(2,1)} %all-gather.4.cloned.1.call-done, bf16[6144,3072]{1,0:T(8,128)(2,1)} %all-gather.6.cloned.1.call-done), kind=kOutput, calls=%fused_computation.29 | convolution fusion | flops 77309411328 | bytes 88080384 | tf_op jit(solution)/shard_map/dot_general | solution.py:22
  556.8 240.9 %all-gather.8.cloned.1.call-done = bf16[3072,6144]{1,0:T(8,128)(2,1)} async-done(((bf16[768,6144]{1,0:T(8,128)(2,1)}), bf16[3072,6144]{1,0:T(8,128)(2,1)}) %all-gather.8.cloned.1.call-update) | async-done | bytes 37748752 | tf_op jit(solution)/shard_map/all_gather | solution.py:20
  797.6 95.1 %fusion.8 = f32[2048,6144]{1,0:T(8,128)} fusion(bf16[3072,6144]{1,0:T(8,128)(2,1)} %all-gather.8.cloned.1.call-done, f32[2048,3072]{1,0:T(8,128)} %fusion.24), kind=kOutput, calls=%fused_computation.9 | convolution fusion | flops 77366034432 | bytes 113246208 | tf_op jit(solution)/shard_map/dot_general | solution.py:24
  892.8 0.0 copy-start
  892.8 0.1 reduce-scatter.2.cloned.1.call-update
  892.8 247.0 %reduce-scatter.2.cloned.1.call-done = f32[256,6144]{1,0:T(8,128)} async-done(((f32[2048,6144]{1,0:T(8,128)}), f32[256,6144]{1,0:T(8,128)}) %reduce-scatter.2.cloned.1.call-update) | async-done | bytes 6291472 | tf_op jit(solution)/shard_map/reduce_scatter | solution.py:25
  1139.9 0.0 copy-done
  1139.9 5.3 fusion.19
  (2 shorter events, 0.0 us)
Async XLA Ops:
  6.5 132.9 %all-gather.4.cloned.1.call-start = ((), (), s32[]{:S(2)}) async-start(), calls=%async_computation.1 | async-start | bytes 28311552 | tf_op jit(solution)/shard_map/all_gather | solution.py:21
  16.7 451.9 %all-gather.6.cloned.1.call-start = ((), (), s32[]{:S(2)}) async-start(), calls=%async_computation.2 | async-start | bytes 47185920 | tf_op jit(solution)/shard_map/all_gather | solution.py:19
  17.5 780.1 %all-gather.8.cloned.1.call-start = ((), (), s32[]{:S(2)}) async-start(), calls=%async_computation.3 | async-start | bytes 47185920 | tf_op jit(solution)/shard_map/all_gather | solution.py:20
  18.3 1121.5 %reduce-scatter.2.cloned.1.call-start = ((), (), s32[]{:S(2)}) async-start(), calls=%async_computation.4 | async-start | bytes 56623104 | tf_op jit(solution)/shard_map/reduce_scatter | solution.py:25
  892.8 247.1 %copy-start = (bf16[256,6144]{1,0:T(8,128)(2,1)S(1)}, bf16[256,6144]{1,0:T(8,128)(2,1)}, u32[]{:S(2)}) copy-start(bf16[256,6144]{1,0:T(8,128)(2,1)} %param.4) | copy-start | bytes 9437188
Sparse Core Ops, SparseCore 0:
  16.8 122.5 all-gather.3
  141.0 327.4 all-gather.5
  470.2 327.4 all-gather.7
  893.0 246.8 reduce-scatter.1
where the time goes:
time: 1150 us
  waiting for transfers between devices  940 us (82%)
  matrix products  183 us (16%)
  other arithmetic  15.4 us (1%)
  between operations  13.2 us (1%)
    all_gather x1, waiting for transfers between devices, local_mlp(): w_in_tp = lax.all_gather(w_in, 'fsdp', axis=0, tiled=True)  329 us
    reduce_scatter x1, waiting for transfers between devices, local_mlp(): mlp_out = lax.psum_scatter(part_sum, 'tp', scatter_dimension=0, tiled=True)  247 us
    all_gather x1, waiting for transfers between devices, local_mlp(): w_out_tp = lax.all_gather(w_out, 'fsdp', axis=0, tiled=True)  241 us
    all_gather x1, waiting for transfers between devices, local_mlp(): group_normed = lax.all_gather(normed, 'tp', axis=0, tiled=True)  121 us
    dot_general x1, matrix products, local_mlp(): part_sum = jnp.dot(act_out, w_out_tp, preferred_element_type=jnp.float32)  95.1 us
    dot_general x1, matrix products, local_mlp(): pre_act = jnp.dot(group_normed, w_in_tp, preferred_element_type=jnp.float32)  88.2 us
  transfers between devices with their start and end apart: 4, of which 4 were waited for; matrix products, arithmetic and copies ran while one was open for 8% of the time, Pallas kernels for 0%

commit v1 on v0

v1 whole, which is shorter than its diff:
```python
import functools

import jax
import jax.numpy as jnp
from jax import lax
from jax.experimental import pallas as pl
from jax.experimental.pallas import tpu as pltpu
from jax.sharding import PartitionSpec as P

LN_EPS = 1e-6
CHUNKS = 12
F32 = jnp.float32
BF16 = jnp.bfloat16


def mlp_kernel(
    n_tp, n_y, N, hid_ref, scale_ref, win_ref, wout_ref, out_ref, gin_ref, gout_ref,
    u_all, h, wbuf, hid_v, own, sibst, sibr, far, near,
    ws_sem, wr_sem, fs_sem, fr_sem, ld_sem, hid_sem, out_sem,
    us_sem, ur_sem, uf_s, uf_r, ub_s, ub_r,
    sb_s, sb_r, far_s, far_r, near_s, near_r,
):
    R, D = hid_v.shape
    Fb = h.shape[1]
    dk, fs = win_ref.shape[0], wout_ref.shape[0]
    cf, cd = Fb // N, D // N
    n_x = n_tp // 2
    t = lax.axis_index("tp")
    y = lax.axis_index("fsdp")
    x, c = lax.div(t, 2), lax.rem(t, 2)
    xr, xl, xf = lax.rem(x + 1, n_x), lax.rem(x + n_x - 1, n_x), lax.rem(x + 2, n_x)
    tr, tl, tf = xr * 2 + c, xl * 2 + c, xf * 2 + c
    tsib = x * 2 + 1 - c
    yr, yl, yf = lax.rem(y + 1, n_y), lax.rem(y + n_y - 1, n_y), lax.rem(y + 2, n_y)
    ynb = ({"fsdp": yr}, {"fsdp": yl})
    xnb = ({"tp": tr}, {"tp": tl})
    sib = {"tp": tsib}

    def remote(src, dst, s, r, dev):
        return pltpu.make_async_remote_copy(
            src_ref=src, dst_ref=dst, send_sem=s, recv_sem=r, device_id=dev, device_id_type=pl.DeviceIdType.MESH
        )

    def cols(k, n):
        return pl.ds(pl.multiple_of(k * n, 128), n)

    def own_copy(ph, k, d):
        if ph == 0:
            src, dst = win_ref.at[:, cols(k, cf)], gin_ref.at[y, :, cols(k, cf)]
        else:
            src, dst = wout_ref.at[:, cols(k, cd)], gout_ref.at[y, :, cols(k, cd)]
        return remote(src, dst, ws_sem.at[ph, lax.rem(k, 2), d], wr_sem.at[ph, k, d], ynb[d])

    def fwd_copy(ph, k, d):
        o = (yl, yr)[d]
        if ph == 0:
            ref = gin_ref.at[o, pl.ds(d * (dk // 2), dk // 2), cols(k, cf)]
        else:
            ref = gout_ref.at[o, pl.ds(d * (fs // 2), fs // 2), cols(k, cd)]
        return remote(ref, ref, fs_sem.at[ph, lax.rem(k, 2), d], fr_sem.at[ph, k, d], ynb[d])

    def start_own(ph, k):
        for d in range(2):
            @pl.when(k >= 2)
            def _():
                own_copy(ph, k - 2, d).wait_send()

            own_copy(ph, k, d).start()

    def forward(ph, k):
        for d in range(2):
            own_copy(ph, k, d).wait_recv()

            @pl.when(k >= 2)
            def _():
                fwd_copy(ph, k - 2, d).wait_send()

            fwd_copy(ph, k, d).start()

    def wait_far(ph, k):
        for d in range(2):
            fwd_copy(ph, k, d).wait_recv()

    def pump(ph, k):
        for fn, a in ((start_own, 2), (forward, 1)):
            @pl.when(k + a < N)
            def _():
                fn(ph, k + a)

            if ph == 0:
                @pl.when(k + a >= N)
                def _():
                    fn(1, k + a - N)
        wait_far(ph, k)

    def drain_sends(ph):
        for k in (N - 2, N - 1):
            for d in range(2):
                own_copy(ph, k, d).wait_send()
                fwd_copy(ph, k, d).wait_send()

    barrier = pltpu.get_barrier_semaphore()
    for dev in (*ynb, *xnb, sib):
        pl.semaphore_signal(barrier, inc=1, device_id=dev, device_id_type=pl.DeviceIdType.MESH)
    hid_load = pltpu.make_async_copy(hid_ref, hid_v, hid_sem)
    hid_load.start()
    pl.semaphore_wait(barrier, 5)

    start_own(0, 0)
    start_own(0, 1)

    hid_load.wait()
    TR = 16

    @pl.loop(0, R // TR)
    def _(i):
        rows = pl.ds(pl.multiple_of(i * TR, TR), TR)
        v = hid_v[rows, :].astype(F32)
        cen = v - jnp.mean(v, axis=-1, keepdims=True)
        var = jnp.mean(cen * cen, axis=-1, keepdims=True)
        u = (cen * lax.rsqrt(var + LN_EPS) * scale_ref[...]).astype(BF16)
        u_all[pl.ds(pl.multiple_of(t * R + i * TR, TR), TR), :] = u

    hr = R // 2

    def urows(tt, part):
        return u_all.at[pl.ds(pl.multiple_of(tt * R + part * hr, 16), hr), :]

    def u_copy(d, part):
        return remote(urows(t, part), urows(t, part), us_sem.at[d, part], ur_sem.at[d, part], xnb[d])

    def u_fwd(d):
        ref = urows((tl, tr)[d], d)
        return remote(ref, ref, uf_s.at[d], uf_r.at[d], xnb[d])

    SIB = ((t, 0), (t, 1), (tl, 0), (tr, 1), (tl, 1), (tr, 0), (tf, 0), (tf, 1))

    def u_sib(i):
        ref = urows(*SIB[i])
        return remote(ref, ref, ub_s.at[i], ub_r.at[i], sib)

    for i in range(2):
        u_copy(0, i).start()
        u_copy(1, 1 - i).start()
    u_sib(0).start()
    u_sib(1).start()

    forward(0, 0)
    pump(0, 0)
    u_copy(0, 0).wait_recv()
    u_fwd(0).start()
    u_copy(1, 1).wait_recv()
    u_fwd(1).start()
    u_sib(2).start()
    u_sib(3).start()
    pump(0, 1)
    u_copy(0, 1).wait_recv()
    u_sib(4).start()
    u_copy(1, 0).wait_recv()
    u_sib(5).start()
    pump(0, 2)
    for d in range(2):
        u_fwd(d).wait_recv()
        u_sib(6 + d).start()

    def up_chunk(k):
        loads = []
        for i, o in enumerate((y, yl, yr, yf)):
            src = win_ref if i == 0 else gin_ref.at[o]
            dst = wbuf.at[
                pl.ds(pl.multiple_of(lax.rem(o, 2) * dk, 16), dk),
                pl.ds(pl.multiple_of(lax.div(o, 2) * cf, 128), cf),
            ]
            loads.append(pltpu.make_async_copy(src.at[:, cols(k, cf)], dst, ld_sem.at[i]))
        for cp in loads:
            cp.start()
        for cp in loads:
            cp.wait()

        @pl.loop(0, n_tp)
        def _(b):
            rows = pl.ds(pl.multiple_of(b * R, 16), R)
            pre = jnp.dot(u_all[rows, : D // 2], wbuf[:, :cf], preferred_element_type=F32)
            pre += jnp.dot(u_all[rows, D // 2 :], wbuf[:, cf:], preferred_element_type=F32)
            h[rows, cols(k, cf)] = jax.nn.gelu(pre, approximate=True).astype(BF16)

    pump(0, 3)
    for i in range(8):
        u_sib(i).wait_recv()

    @pl.loop(0, 3)
    def _(i):
        @pl.when(i > 0)
        def _():
            pump(0, i + 3)

        @pl.loop(0, 2)
        def _(b):
            up_chunk(2 * i + b)

    @pl.loop(6, N)
    def _(k):
        pump(0, k)
        up_chunk(k)

    drain_sends(0)
    for d in range(2):
        u_fwd(d).wait_send()
        for part in range(2):
            u_copy(d, part).wait_send()
    for i in range(8):
        u_sib(i).wait_send()

    hc = cd // 2

    def sib_copy(j):
        s = lax.rem(j, 2)
        return remote(sibst, sibr.at[s], sb_s, sb_r.at[s], sib)

    def far_copy(j, d):
        s = lax.rem(j, 2)
        return remote(
            own.at[lax.rem(j, 3), xf, :, pl.ds(d * hc, hc)], far.at[s, d], far_s.at[s, d], far_r.at[s, d], xnb[d]
        )

    def near_copy(j, d):
        s = lax.rem(j, 2)
        return remote(own.at[lax.rem(j, 3), (xr, xl)[d]], near.at[s, d], near_s.at[s, d], near_r.at[s, d], xnb[d])

    def out_copy(j):
        return pltpu.make_async_copy(hid_v.at[:, cols(j, cd)], out_ref.at[:, cols(j, cd)], out_sem.at[j])

    def down_chunk(j):
        loads = []
        for i, o in enumerate((y, yl, yr, yf)):
            src = wout_ref if i == 0 else gout_ref.at[o]
            dst = wbuf.at[pl.ds(pl.multiple_of(o * fs, 16), fs), :]
            loads.append(pltpu.make_async_copy(src.at[:, cols(j, cd)], dst, ld_sem.at[i]))
        for cp in loads:
            cp.start()

        @pl.when(j >= 1)
        def _():
            sib_copy(j - 1).wait_send()

        for cp in loads:
            cp.wait()

        @pl.loop(0, n_x)
        def _(b):
            rows = pl.ds(pl.multiple_of((b * 2 + 1 - c) * R, 16), R)
            sibst[b] = jnp.dot(h[rows, :], wbuf[...], preferred_element_type=F32)

        sib_copy(j).start()
        s3 = lax.rem(j, 3)

        @pl.loop(0, n_x)
        def _(b):
            rows = pl.ds(pl.multiple_of((b * 2 + c) * R, 16), R)
            own[s3, b] = jnp.dot(h[rows, :], wbuf[...], preferred_element_type=F32)

    def reduce_pair(j):
        s3, s2 = lax.rem(j, 3), lax.rem(j, 2)
        sib_copy(j).wait_recv()

        @pl.loop(0, n_x)
        def _(b):
            own[s3, b] = own[s3, b] + sibr[s2, b]

        for d in range(2):
            @pl.when(j >= 2)
            def _():
                far_copy(j - 2, d).wait_send()

            far_copy(j, d).start()

    def reduce_far(j):
        s3, s2 = lax.rem(j, 3), lax.rem(j, 2)
        for d in range(2):
            half = slice(d * hc, (d + 1) * hc)
            far_copy(j, d).wait_recv()
            b = (xr, xl)[d]
            own[s3, b, :, half] = own[s3, b, :, half] + far[s2, d]
        for d in range(2):
            @pl.when(j >= 2)
            def _():
                near_copy(j - 2, d).wait_send()

            near_copy(j, d).start()

    def finish(j):
        s3, s2 = lax.rem(j, 3), lax.rem(j, 2)
        for d in range(2):
            near_copy(j, d).wait_recv()
        tot = own[s3, x] + near[s2, 0] + near[s2, 1]
        hid_v[:, cols(j, cd)] = (hid_v[:, cols(j, cd)].astype(F32) + tot).astype(BF16)
        out_copy(j).start()

    @pl.loop(0, N)
    def _(j):
        pump(1, j)

        @pl.when(j >= 1)
        def _():
            reduce_far(j - 1)

        @pl.when(j >= 2)
        def _():
            finish(j - 2)

        down_chunk(j)
        reduce_pair(j)

    reduce_far(N - 1)
    finish(N - 2)
    finish(N - 1)

    drain_sends(1)
    sib_copy(N - 1).wait_send()
    for d in range(2):
        for j in (N - 2, N - 1):
            far_copy(j, d).wait_send()
            near_copy(j, d).wait_send()
    for j in range(N):
        out_copy(j).wait()


def make_local(n_tp, n_y, N):
    def local_mlp(hidden, ln_scale, w_in, w_out):
        R, D = hidden.shape
        dk, Fb = w_in.shape
        fs = w_out.shape[0]
        cd = D // N
        any_spec = pl.BlockSpec(memory_space=pl.ANY)
        dma = pltpu.SemaphoreType.DMA
        flops = 4 * n_tp * R * D * Fb
        out, _, _ = pl.pallas_call(
            functools.partial(mlp_kernel, n_tp, n_y, N),
            out_shape=(
                jax.ShapeDtypeStruct((R, D), BF16),
                jax.ShapeDtypeStruct((n_y, dk, Fb), BF16),
                jax.ShapeDtypeStruct((n_y, fs, D), BF16),
            ),
            in_specs=[any_spec, pl.BlockSpec(memory_space=pltpu.VMEM), any_spec, any_spec],
            out_specs=(any_spec, any_spec, any_spec),
            scratch_shapes=[
                pltpu.VMEM((n_tp * R, D), BF16),
                pltpu.VMEM((n_tp * R, Fb), BF16),
                pltpu.VMEM((Fb, cd), BF16),
                pltpu.VMEM((R, D), BF16),
                pltpu.VMEM((3, n_tp // 2, R, cd), F32),
                pltpu.VMEM((n_tp // 2, R, cd), F32),
                pltpu.VMEM((2, n_tp // 2, R, cd), F32),
                pltpu.VMEM((2, 2, R, cd // 2), F32),
                pltpu.VMEM((2, 2, R, cd), F32),
                dma((2, 2, 2)), dma((2, N, 2)), dma((2, 2, 2)), dma((2, N, 2)), dma((4,)), dma, dma((N,)),
                dma((2, 2)), dma((2, 2)), dma((2,)), dma((2,)), dma((8,)), dma((8,)),
                dma, dma((2,)), dma((2, 2)), dma((2, 2)), dma((2, 2)), dma((2, 2)),
            ],
            compiler_params=pltpu.CompilerParams(
                collective_id=0, has_side_effects=True, vmem_limit_bytes=67043328
            ),
            cost_estimate=pl.CostEstimate(flops=flops, bytes_accessed=8 * D * Fb, transcendentals=0),
            name="mlp",
        )(hidden, ln_scale.reshape(1, D), w_in, w_out)
        return out

    return local_mlp


def solution(mesh):
    return jax.shard_map(
        make_local(mesh.shape["tp"], mesh.shape["fsdp"], CHUNKS),
        mesh=mesh,
        in_specs=(P(("data", "fsdp", "tp"), None), P(None), P("fsdp", "tp"), P(("tp", "fsdp"), None)),
        out_specs=P(("data", "fsdp", "tp"), None),
        check_vma=False,
    )
```

time: 1150 us -> 665 us (0.58)
  waiting for transfers between devices: 940 us -> 0 us
  Pallas kernels: 0 us -> 661 us
  matrix products: 183 us -> 0 us
  other arithmetic: 15.4 us -> 0 us
  between operations: 13.2 us -> 0.01 us
    all_gather x3 -> x0, waiting for transfers between devices: 691 us -> none  [the longest x1 329 us: local_mlp(): w_in_tp = lax.all_gather(w_in, 'fsdp', axis=0, tiled=True)]
    pallas_call x0 -> x1, Pallas kernels: none -> 661 us  [local_mlp(): pl.pallas_call(functools.partial(mlp_kernel, n_tp, n_y, N), out_shape=(ja...]
    reduce_scatter x1 -> x0, waiting for transfers between devices: 247 us -> none  [local_mlp(): mlp_out = lax.psum_scatter(part_sum, 'tp', scatter_dimension=0, tiled=True)]
    dot_general x2 -> x0, matrix products: 183 us -> none  [the longest x1 95.1 us: local_mlp(): part_sum = jnp.dot(act_out, w_out_tp, preferred_element_type=jnp.float32)]
  transfers between devices with their start and end apart: 4 -> 0, of which waited for: 4 -> 0; matrix products, arithmetic and copies ran while one was open for 8% -> 0% of each run, Pallas kernels for 0% -> 0%
where the time goes in v1:
time: 665 us
  Pallas kernels  661 us (99%)
    pallas_call x1, Pallas kernels, local_mlp(): pl.pallas_call(functools.partial(mlp_kernel, n_tp, n_y, N), out_shape=(ja...  661 us

profile of v1, /device:TPU:97, one launch (start us, length us, event | category | flops | bytes accessed | tf_op | source)
XLA Modules:
  0.0 664.7 jit_solution(11326229816578383965)
XLA Ops:
  0.0 660.8 %mlp.1 = (bf16[256,6144]{1,0:T(8,128)(2,1)}, bf16[4,1536,3072]{2,1,0:T(8,128)(2,1)}, bf16[4,768,6144]{2,1,0:T(8,128)(2,1)}) custom-call(bf16[256,6144]{1,0:T(8,128)(2,1)} %hid_ref.1, f32[1,6144]{1,0:T(1,128)} %bitcast.1, bf16[1536,3072]{1,0:T(8,128)(2,1)} %win_ref.1, bf16[768,6144]{1,0:T(8,128)(2,1)} %wout_ref.1), custom_call_target="tpu_custom_call" | custom-call | flops 154618822656 | bytes 150994944 | tf_op jit(solution)/shard_map/mlp/pallas_call | solution.py:337
  660.8 3.9 copy.6

commit v2 on v0

v2 whole, which is shorter than its diff:
```python
import functools

import jax
import jax.numpy as jnp
from jax import lax
from jax.experimental import pallas as pl
from jax.experimental.pallas import tpu as pltpu
from jax.sharding import PartitionSpec as P

LN_EPS = 1e-6
CHUNKS = 24
F32 = jnp.float32
BF16 = jnp.bfloat16
SLOTS = 4


def split_rows(R):
    return R * 9 // 16 // 16 * 16


def mlp_kernel(
    n_tp, n_y, N, hid_ref, scale_ref, win_ref, wout_ref, out_ref, u_ref, gout_ref,
    wb, h, ub, hid_v, own, sibst, sibr, yey, fx, nx, fy, ny, yex,
    hid_sem, ust_sem, ld_sem, w2_sem, out_sem,
    d_s, d_r, s_s, s_r, f_s, f_r, wo_s, wo_r,
    uy_s, uy_r, ux_s, ux_r, uf_s, uf_r, ub_s, ub_r,
    sb_s, sb_r, yey_s, yey_r, fx_s, fx_r, nx_s, nx_r, fy_s, fy_r, ny_s, ny_r, yex_s, yex_r,
):
    R, D = hid_v.shape
    sub = wout_ref.shape[0]
    dk = win_ref.shape[0]
    K1 = 6
    cf, cd = sub // 3, D // N
    F2 = 2 * sub
    n_x = n_tp // 2
    RX = split_rows(R)
    hx, hy = RX // 2, (R - RX) // 2
    t = lax.axis_index("tp")
    y = lax.axis_index("fsdp")
    x, c = lax.div(t, 2), lax.rem(t, 2)
    xr, xl, xf = lax.rem(x + 1, n_x), lax.rem(x + n_x - 1, n_x), lax.rem(x + 2, n_x)
    tr, tl, tf = xr * 2 + c, xl * 2 + c, xf * 2 + c
    tsib = x * 2 + 1 - c
    yp = lax.div(y, 2) * 2 + 1 - lax.rem(y, 2)
    yd = n_y - 1 - y
    yo = n_y - 1 - yp
    pair, other, sib = {"fsdp": yp}, {"fsdp": yd}, {"tp": tsib}
    xnb = ({"tp": tr}, {"tp": tl})

    def remote(src, dst, s, r, dev):
        return pltpu.make_async_remote_copy(
            src_ref=src, dst_ref=dst, send_sem=s, recv_sem=r, device_id=dev, device_id_type=pl.DeviceIdType.MESH
        )

    def cols(k, n):
        return pl.ds(pl.multiple_of(k * n, 128), n)

    def wrows(o):
        return pl.ds(pl.multiple_of(o * dk, 16), dk)

    def sseq(m):
        return lax.rem(m, 2) * 3 + lax.div(m, 2)

    def kseq(m):
        return lax.rem(m + 1, 2) * 3 + lax.div(m, 2)

    def win_cols(first, second, k):
        s = jnp.where(k < 3, first, second) if not isinstance(k, int) else (first if k < 3 else second)
        return pl.ds(pl.multiple_of(s * sub + lax.rem(k, 3) * cf, 128), cf)

    def own_w(k):
        return pltpu.make_async_copy(
            win_ref.at[:, win_cols(y, yd, k)], wb.at[wrows(y), cols(k, cf)], ld_sem.at[2 + k]
        )

    def d_copy(k):
        return remote(
            win_ref.at[:, win_cols(yd, y, k)], wb.at[wrows(y), cols(k, cf)], d_s.at[k], d_r.at[k], other
        )

    def s_copy(k):
        return remote(
            win_ref.at[:, win_cols(yp, yo, k)], wb.at[wrows(y), cols(k, cf)], s_s.at[k], s_r.at[k], pair
        )

    def f_copy(k):
        kk = lax.rem(k + 3, K1)
        return remote(
            wb.at[wrows(yp), cols(k, cf)], wb.at[wrows(yp), cols(kk, cf)], f_s.at[kk], f_r.at[kk], other
        )

    def f_recv(k):
        return remote(wb.at[wrows(yo), cols(k, cf)], wb.at[wrows(yo), cols(k, cf)], f_s.at[k], f_r.at[k], other)

    def wo_copy(j):
        return remote(wout_ref.at[:, cols(j, cd)], gout_ref.at[:, cols(j, cd)], wo_s.at[j], wo_r.at[j], other)

    barrier = pltpu.get_barrier_semaphore()
    for dev in (pair, other, *xnb, sib):
        pl.semaphore_signal(barrier, inc=1, device_id=dev, device_id_type=pl.DeviceIdType.MESH)
    hid_load = pltpu.make_async_copy(hid_ref, hid_v, hid_sem)
    hid_load.start()
    pl.semaphore_wait(barrier, 5)

    s_copy(0).start()
    for m in range(K1):
        d_copy(((m + 1) % 2) * 3 + m // 2).start()

    hid_load.wait()
    TR = 16

    @pl.loop(0, R // TR)
    def _(i):
        rows = pl.ds(pl.multiple_of(i * TR, TR), TR)
        v = hid_v[rows, :].astype(F32)
        cen = v - jnp.mean(v, axis=-1, keepdims=True)
        var = jnp.mean(cen * cen, axis=-1, keepdims=True)
        ub[0, rows, :] = (cen * lax.rsqrt(var + LN_EPS) * scale_ref[...]).astype(BF16)

    u_store = pltpu.make_async_copy(ub.at[0], u_ref.at[0, t], ust_sem)
    u_store.start()
    u_store.wait()

    hr = R // 2

    def urows(yy, tt, part):
        return u_ref.at[yy, tt, pl.ds(part * hr, hr), :]

    def u_pair(part):
        return remote(urows(0, t, part), urows(1, t, part), uy_s.at[part], uy_r.at[part], pair)

    def u_copy(yy, d, part):
        ref = urows(yy, t, part)
        return remote(ref, ref, ux_s.at[yy, d, part], ux_r.at[yy, d, part], xnb[d])

    def u_fwd(yy, d):
        ref = urows(yy, (tl, tr)[d], d)
        return remote(ref, ref, uf_s.at[yy, d], uf_r.at[yy, d], xnb[d])

    SIB = ((t, 0), (t, 1), (tl, 0), (tr, 1), (tl, 1), (tr, 0), (tf, 0), (tf, 1))

    def u_sib(yy, i):
        ref = urows(yy, *SIB[i])
        return remote(ref, ref, ub_s.at[yy, i], ub_r.at[yy, i], sib)

    def u_start(yy):
        for i in range(2):
            u_copy(yy, 0, i).start()
            u_copy(yy, 1, 1 - i).start()

    def u_first(yy):
        u_copy(yy, 0, 0).wait_recv()
        u_fwd(yy, 0).start()
        u_copy(yy, 1, 1).wait_recv()
        u_fwd(yy, 1).start()
        u_sib(yy, 2).start()
        u_sib(yy, 3).start()

    def u_second(yy):
        u_copy(yy, 0, 1).wait_recv()
        u_sib(yy, 4).start()
        u_copy(yy, 1, 0).wait_recv()
        u_sib(yy, 5).start()

    def u_third(yy):
        for d in range(2):
            u_fwd(yy, d).wait_recv()
            u_sib(yy, 6 + d).start()

    u_start(0)
    for i in range(2):
        u_pair(i).start()
        u_sib(0, i).start()
    for m in range(1, K1):
        s_copy((m % 2) * 3 + m // 2).start()
    for k in range(K1):
        own_w(k).start()

    def block(i):
        yy = lax.div(i, n_tp)
        m = lax.div(lax.rem(i, n_tp), 2)
        off = lax.div(m * (m + 1), 2)
        return yy, lax.rem(x + off, n_x) * 2 + lax.rem(i, 2)

    def u_load(i):
        yy, tt = block(i)
        return pltpu.make_async_copy(u_ref.at[yy, tt], ub.at[lax.rem(i, 2)], ld_sem.at[lax.rem(i, 2)])

    def up(i0, i1, m0, m1):
        u_load(i0).start()

        @pl.loop(i0, i1)
        def _(i):
            @pl.when(i + 1 < i1)
            def _():
                u_load(i + 1).start()

            u_load(i).wait()
            yy, tt = block(i)
            rows = pl.ds(pl.multiple_of((yy * n_tp + tt) * R, 16), R)

            @pl.loop(m0, m1)
            def _(m):
                k = kseq(m)
                pre = jnp.dot(ub[lax.rem(i, 2)], wb[:, cols(k, cf)], preferred_element_type=F32)
                h[rows, cols(k, cf)] = jax.nn.gelu(pre, approximate=True).astype(BF16)

    def s_event(m):
        s_copy(sseq(m)).wait_recv()
        f_copy(sseq(m)).start()

    def w_ready(m):
        k = kseq(m)
        d_copy(k).wait_recv()
        f_recv(k).wait_recv()

    s_event(0)
    u_first(0)
    u_second(0)
    for i in range(2):
        u_pair(i).wait_recv()
    u_start(1)
    for i in range(2):
        u_sib(1, i).start()
    s_event(1)
    u_third(0)
    for i in range(8):
        u_sib(0, i).wait_recv()
    for i in range(2):
        u_sib(1, i).wait_recv()
    for k in range(K1):
        own_w(k).wait()

    @pl.loop(0, 4)
    def _(m):
        s_event(m + 2)
        w_ready(m)

        @pl.when(m == 2)
        def _():
            u_first(1)

        up(0, 10, m, m + 1)

    for j in range(SLOTS):
        wo_copy(j).start()
    u_second(1)
    for i in range(2, 6):
        u_sib(1, i).wait_recv()
    up(10, 14, 0, 4)

    @pl.loop(4, K1)
    def _(m):
        w_ready(m)
        up(0, 14, m, m + 1)

    u_third(1)
    for i in range(6, 8):
        u_sib(1, i).wait_recv()
    up(14, 16, 0, K1)

    for k in range(K1):
        f_copy(k).wait_send()
        d_copy(k).wait_send()
        s_copy(k).wait_send()

    def s2(j):
        return lax.rem(j, 2)

    def s4(j):
        return lax.rem(j, SLOTS)

    def sib_copy(j):
        return remote(sibst, sibr.at[s2(j)], sb_s, sb_r.at[s2(j)], sib)

    def yey_copy(j):
        return remote(own.at[s4(j), 1, :, pl.ds(RX, R - RX)], yey.at[s4(j)], yey_s.at[s2(j)], yey_r.at[s4(j)], pair)

    def yex_copy(j):
        return remote(own.at[s4(j), 1, x, pl.ds(0, RX)], yex.at[s4(j)], yex_s.at[s2(j)], yex_r.at[s4(j)], pair)

    def fx_copy(j, d):
        src = own.at[s4(j), :, xf, pl.ds(d * hx, hx)]
        return remote(src, fx.at[s4(j), d], fx_s.at[s2(j), d], fx_r.at[s4(j), d], xnb[d])

    def nx_copy(j, d):
        src = own.at[s4(j), :, (xr, xl)[d], pl.ds(0, RX)]
        return remote(src, nx.at[s4(j), d], nx_s.at[s2(j), d], nx_r.at[s4(j), d], xnb[d])

    def fy_copy(j, d):
        src = own.at[s4(j), 0, xf, pl.ds(RX + d * hy, hy)]
        return remote(src, fy.at[s4(j), d], fy_s.at[s2(j), d], fy_r.at[s4(j), d], xnb[d])

    def ny_copy(j, d):
        src = own.at[s4(j), 0, (xr, xl)[d], pl.ds(RX, R - RX)]
        return remote(src, ny.at[s4(j), d], ny_s.at[s2(j), d], ny_r.at[s4(j), d], xnb[d])

    def out_copy(j):
        return pltpu.make_async_copy(hid_v.at[:, cols(j, cd)], out_ref.at[:, cols(j, cd)], out_sem.at[j])

    def send(copy, j, *a):
        @pl.when(j >= 2)
        def _():
            copy(j - 2, *a).wait_send()

        copy(j, *a).start()

    def w2_loads(j):
        dst = wb.at[:, cols(s2(j), cd)]
        return (
            pltpu.make_async_copy(wout_ref.at[:, cols(j, cd)], dst.at[pl.ds(0, sub)], w2_sem.at[s2(j), 0]),
            pltpu.make_async_copy(gout_ref.at[:, cols(j, cd)], dst.at[pl.ds(sub, sub)], w2_sem.at[s2(j), 1]),
        )

    def fetch(j):
        wo_copy(j).wait_recv()
        for cp in w2_loads(j):
            cp.start()

    def down(j):
        for cp in w2_loads(j):
            cp.wait()

        @pl.when(j + 1 < N)
        def _():
            fetch(j + 1)

        @pl.when(j >= 1)
        def _():
            sib_copy(j - 1).wait_send()

        def part(i, cc):
            yy, xx = lax.div(i, n_x), lax.rem(i, n_x)
            rows = pl.ds(pl.multiple_of((yy * n_tp + xx * 2 + cc) * R, 16), R)
            return jnp.dot(h[rows, :], wb[:F2, cols(s2(j), cd)], preferred_element_type=F32)

        @pl.loop(0, 2 * n_x)
        def _(i):
            sibst[lax.div(i, n_x), lax.rem(i, n_x)] = part(i, 1 - c)

        sib_copy(j).start()

        @pl.loop(0, 2 * n_x)
        def _(i):
            own[s4(j), lax.div(i, n_x), lax.rem(i, n_x)] = part(i, c)

    def stage1(j):
        sib_copy(j).wait_recv()

        @pl.loop(0, 2 * n_x)
        def _(i):
            yy, xx = lax.div(i, n_x), lax.rem(i, n_x)
            own[s4(j), yy, xx] = own[s4(j), yy, xx] + sibr[s2(j), yy, xx]

        send(yey_copy, j)
        for d in range(2):
            send(fx_copy, j, d)

    def stage2(j):
        s = s4(j)
        for d in range(2):
            fx_copy(j, d).wait_recv()
            b, rows = (xr, xl)[d], slice(d * hx, (d + 1) * hx)
            for yy in range(2):
                own[s, yy, b, rows] = own[s, yy, b, rows] + fx[s, d, yy]
        for d in range(2):
            send(nx_copy, j, d)
        yey_copy(j).wait_recv()

        @pl.loop(0, n_x)
        def _(i):
            own[s, 0, i, RX:] = own[s, 0, i, RX:] + yey[s, i]

        for d in range(2):
            send(fy_copy, j, d)

    def stage3(j):
        s = s4(j)
        for d in range(2):
            fy_copy(j, d).wait_recv()
            b, rows = (xr, xl)[d], slice(RX + d * hy, RX + (d + 1) * hy)
            own[s, 0, b, rows] = own[s, 0, b, rows] + fy[s, d]
        for d in range(2):
            ny_copy(j, d).start()
        for d in range(2):
            nx_copy(j, d).wait_recv()
        for yy in (1, 0):
            own[s, yy, x, :RX] = own[s, yy, x, :RX] + nx[s, 0, yy] + nx[s, 1, yy]
        yex_copy(j).start()

    def stage4(j):
        s = s4(j)
        for d in range(2):
            ny_copy(j, d).wait_recv()
        lo = own[s, 0, x, RX:] + ny[s, 0] + ny[s, 1]
        hid_v[RX:, cols(j, cd)] = (hid_v[RX:, cols(j, cd)].astype(F32) + lo).astype(BF16)
        yex_copy(j).wait_recv()
        hi = own[s, 0, x, :RX] + yex[s]
        hid_v[:RX, cols(j, cd)] = (hid_v[:RX, cols(j, cd)].astype(F32) + hi).astype(BF16)
        out_copy(j).start()
        yex_copy(j).wait_send()
        for d in range(2):
            ny_copy(j, d).wait_send()

    fetch(0)

    @pl.loop(0, N + 3)
    def _(j):
        @pl.when(j + SLOTS < N)
        def _():
            wo_copy(j + SLOTS).start()

        @pl.when(j < N)
        def _():
            down(j)
            stage1(j)

        @pl.when(jnp.logical_and(j >= 1, j < N + 1))
        def _():
            stage2(j - 1)

        @pl.when(jnp.logical_and(j >= 2, j < N + 2))
        def _():
            stage3(j - 2)

        @pl.when(j >= 3)
        def _():
            stage4(j - 3)

    for yy in range(2):
        for d in range(2):
            u_fwd(yy, d).wait_send()
            for part in range(2):
                u_copy(yy, d, part).wait_send()
        for i in range(8):
            u_sib(yy, i).wait_send()
    for part in range(2):
        u_pair(part).wait_send()
    sib_copy(N - 1).wait_send()
    for j in (N - 2, N - 1):
        yey_copy(j).wait_send()
        for d in range(2):
            for copy in (fx_copy, nx_copy, fy_copy):
                copy(j, d).wait_send()

    @pl.loop(0, N)
    def _(j):
        wo_copy(j).wait_send()
        out_copy(j).wait()


def make_local(n_tp, n_y, N):
    def local_mlp(hidden, ln_scale, w_in, w_out):
        R, D = hidden.shape
        sub = w_out.shape[0]
        cd = D // N
        n_x = n_tp // 2
        RX = split_rows(R)
        any_spec = pl.BlockSpec(memory_space=pl.ANY)
        dma = pltpu.SemaphoreType.DMA
        vm = pltpu.VMEM
        S = SLOTS
        out, _, _ = pl.pallas_call(
            functools.partial(mlp_kernel, n_tp, n_y, N),
            out_shape=(
                jax.ShapeDtypeStruct((R, D), BF16),
                jax.ShapeDtypeStruct((2, n_tp, R, D), BF16),
                jax.ShapeDtypeStruct((sub, D), BF16),
            ),
            in_specs=[any_spec, pl.BlockSpec(memory_space=vm), any_spec, any_spec],
            out_specs=(any_spec, any_spec, any_spec),
            scratch_shapes=[
                vm((D, 2 * sub), BF16),
                vm((2 * n_tp * R, 2 * sub), BF16),
                vm((2, R, D), BF16),
                vm((R, D), BF16),
                vm((S, 2, n_x, R, cd), F32),
                vm((2, n_x, R, cd), F32),
                vm((2, 2, n_x, R, cd), F32),
                vm((S, n_x, R - RX, cd), F32),
                vm((S, 2, 2, RX // 2, cd), F32),
                vm((S, 2, 2, RX, cd), F32),
                vm((S, 2, (R - RX) // 2, cd), F32),
                vm((S, 2, R - RX, cd), F32),
                vm((S, RX, cd), F32),
                dma, dma, dma((8,)), dma((2, 2)), dma((N,)),
                dma((6,)), dma((6,)), dma((6,)), dma((6,)), dma((6,)), dma((6,)), dma((N,)), dma((N,)),
                dma((2,)), dma((2,)), dma((2, 2, 2)), dma((2, 2, 2)), dma((2, 2)), dma((2, 2)), dma((2, 8)), dma((2, 8)),
                dma, dma((2,)), dma((2,)), dma((S,)), dma((2, 2)), dma((S, 2)), dma((2, 2)), dma((S, 2)),
                dma((2, 2)), dma((S, 2)), dma((2, 2)), dma((S, 2)), dma((2,)), dma((S,)),
            ],
            compiler_params=pltpu.CompilerParams(
                collective_id=0, has_side_effects=True, vmem_limit_bytes=67043328
            ),
            cost_estimate=pl.CostEstimate(
                flops=4 * n_tp * R * D * w_in.shape[1], bytes_accessed=8 * D * w_in.shape[1], transcendentals=0
            ),
            name="mlp",
        )(hidden, ln_scale.reshape(1, D), w_in, w_out)
        return out

    return local_mlp


def solution(mesh):
    return jax.shard_map(
        make_local(mesh.shape["tp"], mesh.shape["fsdp"], CHUNKS),
        mesh=mesh,
        in_specs=(P(("data", "fsdp", "tp"), None), P(None), P("fsdp", "tp"), P(("tp", "fsdp"), None)),
        out_specs=P(("data", "fsdp", "tp"), None),
        check_vma=False,
    )
```

time: 1150 us -> 624 us (0.54)
  waiting for transfers between devices: 940 us -> 0 us
  Pallas kernels: 0 us -> 617 us
  matrix products: 183 us -> 0 us
  other arithmetic: 15.4 us -> 0 us
  between operations: 13.2 us -> 0.01 us
    all_gather x3 -> x0, waiting for transfers between devices: 691 us -> none  [the longest x1 329 us: local_mlp(): w_in_tp = lax.all_gather(w_in, 'fsdp', axis=0, tiled=True)]
    pallas_call x0 -> x1, Pallas kernels: none -> 617 us  [local_mlp(): pl.pallas_call(functools.partial(mlp_kernel, n_tp, n_y, N), out_shape=(ja...]
    reduce_scatter x1 -> x0, waiting for transfers between devices: 247 us -> none  [local_mlp(): mlp_out = lax.psum_scatter(part_sum, 'tp', scatter_dimension=0, tiled=True)]
    dot_general x2 -> x0, matrix products: 183 us -> none  [the longest x1 95.1 us: local_mlp(): part_sum = jnp.dot(act_out, w_out_tp, preferred_element_type=jnp.float32)]
  transfers between devices with their start and end apart: 4 -> 0, of which waited for: 4 -> 0; matrix products, arithmetic and copies ran while one was open for 8% -> 0% of each run, Pallas kernels for 0% -> 0%
where the time goes in v2:
time: 624 us; the launch traced here: 621 us
  Pallas kernels  617 us (99%)
    pallas_call x1, Pallas kernels, local_mlp(): pl.pallas_call(functools.partial(mlp_kernel, n_tp, n_y, N), out_shape=(ja...  617 us

profile of v2, /device:TPU:97, one launch (start us, length us, event | category | flops | bytes accessed | tf_op | source)
XLA Modules:
  0.0 620.8 jit_solution(995584495426971062)
XLA Ops:
  0.0 617.0 %mlp.1 = (bf16[256,6144]{1,0:T(8,128)(2,1)}, bf16[2,8,256,6144]{3,2,1,0:T(8,128)(2,1)}, bf16[768,6144]{1,0:T(8,128)(2,1)}) custom-call(bf16[256,6144]{1,0:T(8,128)(2,1)} %hid_ref.1, f32[1,6144]{1,0:T(1,128)} %bitcast.1, bf16[1536,3072]{1,0:T(8,128)(2,1)} %win_ref.1, bf16[768,6144]{1,0:T(8,128)(2,1)} %wout_ref.1), custom_call_target="tpu_custom_call" | custom-call | flops 154618822656 | bytes 150994944 | tf_op jit(solution)/shard_map/mlp/pallas_call | solution.py:463
  617.0 3.9 copy.6

commit v3 on v2

--- a/solution.py
+++ b/solution.py
@@ -21,7 +21,7 @@
 def mlp_kernel(
     n_tp, n_y, N, hid_ref, scale_ref, win_ref, wout_ref, out_ref, u_ref, gout_ref,
     wb, h, ub, hid_v, own, sibst, sibr, yey, fx, nx, fy, ny, yex,
-    hid_sem, ust_sem, ld_sem, w2_sem, out_sem,
+    hid_sem, ust_sem, ld_sem, ow_sem, w2_sem, out_sem,
     d_s, d_r, s_s, s_r, f_s, f_r, wo_s, wo_r,
     uy_s, uy_r, ux_s, ux_r, uf_s, uf_r, ub_s, ub_r,
     sb_s, sb_r, yey_s, yey_r, fx_s, fx_r, nx_s, nx_r, fy_s, fy_r, ny_s, ny_r, yex_s, yex_r,
@@ -70,7 +70,7 @@
 
     def own_w(k):
         return pltpu.make_async_copy(
-            win_ref.at[:, win_cols(y, yd, k)], wb.at[wrows(y), cols(k, cf)], ld_sem.at[2 + k]
+            win_ref.at[:, win_cols(y, yd, k)], wb.at[wrows(y), cols(k, cf)], ow_sem.at[k]
         )
 
     def d_copy(k):
@@ -98,40 +98,48 @@
     barrier = pltpu.get_barrier_semaphore()
     for dev in (pair, other, *xnb, sib):
         pl.semaphore_signal(barrier, inc=1, device_id=dev, device_id_type=pl.DeviceIdType.MESH)
-    hid_load = pltpu.make_async_copy(hid_ref, hid_v, hid_sem)
-    hid_load.start()
+
+    def hid_load(part):
+        rows = pl.ds(part * (R // 2), R // 2)
+        return pltpu.make_async_copy(hid_ref.at[rows], hid_v.at[rows], hid_sem.at[part])
+
+    for part in range(2):
+        hid_load(part).start()
     pl.semaphore_wait(barrier, 5)
 
     s_copy(0).start()
     for m in range(K1):
         d_copy(((m + 1) % 2) * 3 + m // 2).start()
 
-    hid_load.wait()
     TR = 16
-
-    @pl.loop(0, R // TR)
-    def _(i):
-        rows = pl.ds(pl.multiple_of(i * TR, TR), TR)
-        v = hid_v[rows, :].astype(F32)
-        cen = v - jnp.mean(v, axis=-1, keepdims=True)
-        var = jnp.mean(cen * cen, axis=-1, keepdims=True)
-        ub[0, rows, :] = (cen * lax.rsqrt(var + LN_EPS) * scale_ref[...]).astype(BF16)
-
-    u_store = pltpu.make_async_copy(ub.at[0], u_ref.at[0, t], ust_sem)
-    u_store.start()
-    u_store.wait()
-
     hr = R // 2
+
+    def normalize(part):
+        hid_load(part).wait()
+
+        @pl.loop(0, hr // TR)
+        def _(i):
+            rows = pl.ds(pl.multiple_of(part * hr + i * TR, TR), TR)
+            v = hid_v[rows, :].astype(F32)
+            cen = v - jnp.mean(v, axis=-1, keepdims=True)
+            var = jnp.mean(cen * cen, axis=-1, keepdims=True)
+            ub[0, rows, :] = (cen * lax.rsqrt(var + LN_EPS) * scale_ref[...]).astype(BF16)
 
     def urows(yy, tt, part):
         return u_ref.at[yy, tt, pl.ds(part * hr, hr), :]
 
+    def uown(part):
+        return ub.at[0, pl.ds(part * hr, hr), :]
+
+    def u_store(part):
+        return pltpu.make_async_copy(uown(part), urows(0, t, part), ust_sem.at[part])
+
     def u_pair(part):
-        return remote(urows(0, t, part), urows(1, t, part), uy_s.at[part], uy_r.at[part], pair)
+        return remote(uown(part), urows(1, t, part), uy_s.at[part], uy_r.at[part], pair)
 
     def u_copy(yy, d, part):
         ref = urows(yy, t, part)
-        return remote(ref, ref, ux_s.at[yy, d, part], ux_r.at[yy, d, part], xnb[d])
+        return remote(uown(part) if yy == 0 else ref, ref, ux_s.at[yy, d, part], ux_r.at[yy, d, part], xnb[d])
 
     def u_fwd(yy, d):
         ref = urows(yy, (tl, tr)[d], d)
@@ -141,7 +149,7 @@
 
     def u_sib(yy, i):
         ref = urows(yy, *SIB[i])
-        return remote(ref, ref, ub_s.at[yy, i], ub_r.at[yy, i], sib)
+        return remote(uown(i) if yy == 0 and i < 2 else ref, ref, ub_s.at[yy, i], ub_r.at[yy, i], sib)
 
     def u_start(yy):
         for i in range(2):
@@ -167,10 +175,17 @@
             u_fwd(yy, d).wait_recv()
             u_sib(yy, 6 + d).start()
 
-    u_start(0)
+    normalize(0)
+    u_copy(0, 0, 0).start()
+    u_pair(0).start()
+    normalize(1)
+    u_copy(0, 1, 1).start()
+    u_copy(0, 0, 1).start()
+    u_copy(0, 1, 0).start()
+    u_pair(1).start()
     for i in range(2):
-        u_pair(i).start()
         u_sib(0, i).start()
+        u_store(i).start()
     for m in range(1, K1):
         s_copy((m % 2) * 3 + m // 2).start()
     for k in range(K1):
@@ -182,27 +197,37 @@
         off = lax.div(m * (m + 1), 2)
         return yy, lax.rem(x + off, n_x) * 2 + lax.rem(i, 2)
 
-    def u_load(i):
-        yy, tt = block(i)
-        return pltpu.make_async_copy(u_ref.at[yy, tt], ub.at[lax.rem(i, 2)], ld_sem.at[lax.rem(i, 2)])
-
-    def up(i0, i1, m0, m1):
-        u_load(i0).start()
-
-        @pl.loop(i0, i1)
-        def _(i):
-            @pl.when(i + 1 < i1)
+    def up(n, blk, m0, m1, event=None):
+        def loads(idx):
+            yy, tt = block(blk(idx))
+            s = lax.rem(idx, 2)
+            return [
+                pltpu.make_async_copy(urows(yy, tt, p), ub.at[s, pl.ds(p * hr, hr), :], ld_sem.at[s, p])
+                for p in range(2)
+            ]
+
+        for cp in loads(0):
+            cp.start()
+
+        @pl.loop(0, n)
+        def _(idx):
+            if event is not None:
+                event(idx)
+
+            @pl.when(idx + 1 < n)
             def _():
-                u_load(i + 1).start()
-
-            u_load(i).wait()
-            yy, tt = block(i)
+                for cp in loads(idx + 1):
+                    cp.start()
+
+            for cp in loads(idx):
+                cp.wait()
+            yy, tt = block(blk(idx))
             rows = pl.ds(pl.multiple_of((yy * n_tp + tt) * R, 16), R)
 
-            @pl.loop(m0, m1)
+            @pl.loop(m0(idx), m1(idx))
             def _(m):
                 k = kseq(m)
-                pre = jnp.dot(ub[lax.rem(i, 2)], wb[:, cols(k, cf)], preferred_element_type=F32)
+                pre = jnp.dot(ub[lax.rem(idx, 2)], wb[:, cols(k, cf)], preferred_element_type=F32)
                 h[rows, cols(k, cf)] = jax.nn.gelu(pre, approximate=True).astype(BF16)
 
     def s_event(m):
@@ -231,33 +256,62 @@
     for k in range(K1):
         own_w(k).wait()
 
-    @pl.loop(0, 4)
-    def _(m):
-        s_event(m + 2)
-        w_ready(m)
-
-        @pl.when(m == 2)
-        def _():
-            u_first(1)
-
-        up(0, 10, m, m + 1)
-
+    for i in range(2):
+        u_store(i).wait()
+        u_pair(i).wait_send()
+        u_sib(0, i).wait_send()
+        for d in range(2):
+            u_copy(0, d, i).wait_send()
+
+    def same(v):
+        return lambda idx: v
+
+    def straight(idx):
+        return idx
+
+    s_event(2)
+    s_event(3)
+    w_ready(0)
+    w_ready(1)
+    up(10, straight, same(0), same(2))
+    s_event(4)
+    w_ready(2)
+    u_first(1)
+    up(10, straight, same(2), same(3))
+    s_event(5)
     for j in range(SLOTS):
         wo_copy(j).start()
+    w_ready(3)
+    up(10, straight, same(3), same(4))
     u_second(1)
+    w_ready(4)
     for i in range(2, 6):
         u_sib(1, i).wait_recv()
-    up(10, 14, 0, 4)
-
-    @pl.loop(4, K1)
-    def _(m):
-        w_ready(m)
-        up(0, 14, m, m + 1)
-
-    u_third(1)
-    for i in range(6, 8):
-        u_sib(1, i).wait_recv()
-    up(14, 16, 0, K1)
+
+    def early(idx):
+        return lax.div(19 - idx, 16)
+
+    def last_event(idx):
+        @pl.when(idx == 4)
+        def _():
+            w_ready(5)
+
+        @pl.when(idx == 11)
+        def _():
+            u_third(1)
+
+        @pl.when(idx == 17)
+        def _():
+            for i in range(6, 8):
+                u_sib(1, i).wait_recv()
+
+    up(
+        20,
+        lambda idx: idx - 4 + 14 * early(idx),
+        lambda idx: (1 - early(idx)) * (4 + lax.div(idx, 14) - 5 * lax.div(idx, 18)),
+        lambda idx: K1 - early(idx),
+        last_event,
+    )
 
     for k in range(K1):
         f_copy(k).wait_send()
@@ -270,133 +324,162 @@
     def s4(j):
         return lax.rem(j, SLOTS)
 
+    def width(j):
+        return cd // 2 if isinstance(j, int) and j >= N - 1 else cd
+
+    def dcols(j):
+        if width(j) == cd:
+            return cols(j, cd)
+        return pl.ds((N - 1) * cd + (j - N + 1) * (cd // 2), cd // 2)
+
+    def narrow(j):
+        return pl.ds(0, width(j))
+
     def sib_copy(j):
-        return remote(sibst, sibr.at[s2(j)], sb_s, sb_r.at[s2(j)], sib)
+        w = narrow(j)
+        return remote(sibst.at[:, :, :, w], sibr.at[s2(j), :, :, :, w], sb_s, sb_r.at[s2(j)], sib)
 
     def yey_copy(j):
-        return remote(own.at[s4(j), 1, :, pl.ds(RX, R - RX)], yey.at[s4(j)], yey_s.at[s2(j)], yey_r.at[s4(j)], pair)
+        w = narrow(j)
+        src = own.at[s4(j), 1, :, pl.ds(RX, R - RX), w]
+        return remote(src, yey.at[s4(j), :, :, w], yey_s.at[s2(j)], yey_r.at[s4(j)], pair)
 
     def yex_copy(j):
-        return remote(own.at[s4(j), 1, x, pl.ds(0, RX)], yex.at[s4(j)], yex_s.at[s2(j)], yex_r.at[s4(j)], pair)
+        w = narrow(j)
+        return remote(own.at[s4(j), 1, x, pl.ds(0, RX), w], yex.at[s4(j), :, w], yex_s.at[s2(j)], yex_r.at[s4(j)], pair)
 
     def fx_copy(j, d):
-        src = own.at[s4(j), :, xf, pl.ds(d * hx, hx)]
-        return remote(src, fx.at[s4(j), d], fx_s.at[s2(j), d], fx_r.at[s4(j), d], xnb[d])
+        w = narrow(j)
+        src = own.at[s4(j), :, xf, pl.ds(d * hx, hx), w]
+        return remote(src, fx.at[s4(j), d, :, :, w], fx_s.at[s2(j), d], fx_r.at[s4(j), d], xnb[d])
 
     def nx_copy(j, d):
-        src = own.at[s4(j), :, (xr, xl)[d], pl.ds(0, RX)]
-        return remote(src, nx.at[s4(j), d], nx_s.at[s2(j), d], nx_r.at[s4(j), d], xnb[d])
+        w = narrow(j)
+        src = own.at[s4(j), :, (xr, xl)[d], pl.ds(0, RX), w]
+        return remote(src, nx.at[s4(j), d, :, :, w], nx_s.at[s2(j), d], nx_r.at[s4(j), d], xnb[d])
 
     def fy_copy(j, d):
-        src = own.at[s4(j), 0, xf, pl.ds(RX + d * hy, hy)]
-        return remote(src, fy.at[s4(j), d], fy_s.at[s2(j), d], fy_r.at[s4(j), d], xnb[d])
+        w = narrow(j)
+        src = own.at[s4(j), 0, xf, pl.ds(RX + d * hy, hy), w]
+        return remote(src, fy.at[s4(j), d, :, w], fy_s.at[s2(j), d], fy_r.at[s4(j), d], xnb[d])
 
     def ny_copy(j, d):
-        src = own.at[s4(j), 0, (xr, xl)[d], pl.ds(RX, R - RX)]
-        return remote(src, ny.at[s4(j), d], ny_s.at[s2(j), d], ny_r.at[s4(j), d], xnb[d])
+        w = narrow(j)
+        src = own.at[s4(j), 0, (xr, xl)[d], pl.ds(RX, R - RX), w]
+        return remote(src, ny.at[s4(j), d, :, w], ny_s.at[s2(j), d], ny_r.at[s4(j), d], xnb[d])
 
     def out_copy(j):
-        return pltpu.make_async_copy(hid_v.at[:, cols(j, cd)], out_ref.at[:, cols(j, cd)], out_sem.at[j])
+        return pltpu.make_async_copy(hid_v.at[:, dcols(j)], out_ref.at[:, dcols(j)], out_sem.at[j])
+
+    def when_static(cond, fn):
+        if isinstance(cond, bool):
+            if cond:
+                fn()
+        else:
+            pl.when(cond)(fn)
 
     def send(copy, j, *a):
-        @pl.when(j >= 2)
-        def _():
-            copy(j - 2, *a).wait_send()
-
+        when_static(j >= 2, lambda: copy(j - 2, *a).wait_send())
         copy(j, *a).start()
 
+    def w2_cols(j):
+        return pl.ds(pl.multiple_of(s2(j) * cd, 128), width(j))
+
     def w2_loads(j):
-        dst = wb.at[:, cols(s2(j), cd)]
+        lo, hi = pl.ds(0, sub), pl.ds(sub, sub)
         return (
-            pltpu.make_async_copy(wout_ref.at[:, cols(j, cd)], dst.at[pl.ds(0, sub)], w2_sem.at[s2(j), 0]),
-            pltpu.make_async_copy(gout_ref.at[:, cols(j, cd)], dst.at[pl.ds(sub, sub)], w2_sem.at[s2(j), 1]),
+            pltpu.make_async_copy(wout_ref.at[:, dcols(j)], wb.at[lo, w2_cols(j)], w2_sem.at[s2(j), 0]),
+            pltpu.make_async_copy(gout_ref.at[:, dcols(j)], wb.at[hi, w2_cols(j)], w2_sem.at[s2(j), 1]),
         )
 
     def fetch(j):
-        wo_copy(j).wait_recv()
+        if not (isinstance(j, int) and j == N):
+            wo_copy(j).wait_recv()
         for cp in w2_loads(j):
             cp.start()
 
     def down(j):
+        W = slice(0, width(j))
         for cp in w2_loads(j):
             cp.wait()
 
-        @pl.when(j + 1 < N)
-        def _():
-            fetch(j + 1)
-
-        @pl.when(j >= 1)
-        def _():
-            sib_copy(j - 1).wait_send()
+        if isinstance(j, int):
+            if j < N:
+                fetch(j + 1)
+        else:
+            pl.when(j + 1 < N - 1)(lambda: fetch(j + 1))
+            pl.when(j + 1 == N - 1)(lambda: fetch(N - 1))
+        when_static(j >= 1, lambda: sib_copy(j - 1).wait_send())
 
         def part(i, cc):
             yy, xx = lax.div(i, n_x), lax.rem(i, n_x)
             rows = pl.ds(pl.multiple_of((yy * n_tp + xx * 2 + cc) * R, 16), R)
-            return jnp.dot(h[rows, :], wb[:F2, cols(s2(j), cd)], preferred_element_type=F32)
+            return jnp.dot(h[rows, :], wb[:F2, w2_cols(j)], preferred_element_type=F32)
 
         @pl.loop(0, 2 * n_x)
         def _(i):
-            sibst[lax.div(i, n_x), lax.rem(i, n_x)] = part(i, 1 - c)
+            sibst[lax.div(i, n_x), lax.rem(i, n_x), :, W] = part(i, 1 - c)
 
         sib_copy(j).start()
 
         @pl.loop(0, 2 * n_x)
         def _(i):
-            own[s4(j), lax.div(i, n_x), lax.rem(i, n_x)] = part(i, c)
+            own[s4(j), lax.div(i, n_x), lax.rem(i, n_x), :, W] = part(i, c)
 
     def stage1(j):
+        W = slice(0, width(j))
         sib_copy(j).wait_recv()
 
         @pl.loop(0, 2 * n_x)
         def _(i):
             yy, xx = lax.div(i, n_x), lax.rem(i, n_x)
-            own[s4(j), yy, xx] = own[s4(j), yy, xx] + sibr[s2(j), yy, xx]
+            own[s4(j), yy, xx, :, W] = own[s4(j), yy, xx, :, W] + sibr[s2(j), yy, xx, :, W]
 
         send(yey_copy, j)
         for d in range(2):
             send(fx_copy, j, d)
 
     def stage2(j):
-        s = s4(j)
+        s, W = s4(j), slice(0, width(j))
         for d in range(2):
             fx_copy(j, d).wait_recv()
             b, rows = (xr, xl)[d], slice(d * hx, (d + 1) * hx)
             for yy in range(2):
-                own[s, yy, b, rows] = own[s, yy, b, rows] + fx[s, d, yy]
+                own[s, yy, b, rows, W] = own[s, yy, b, rows, W] + fx[s, d, yy, :, W]
         for d in range(2):
             send(nx_copy, j, d)
         yey_copy(j).wait_recv()
 
         @pl.loop(0, n_x)
         def _(i):
-            own[s, 0, i, RX:] = own[s, 0, i, RX:] + yey[s, i]
+            own[s, 0, i, RX:, W] = own[s, 0, i, RX:, W] + yey[s, i, :, W]
 
         for d in range(2):
             send(fy_copy, j, d)
 
     def stage3(j):
-        s = s4(j)
+        s, W = s4(j), slice(0, width(j))
         for d in range(2):
             fy_copy(j, d).wait_recv()
             b, rows = (xr, xl)[d], slice(RX + d * hy, RX + (d + 1) * hy)
-            own[s, 0, b, rows] = own[s, 0, b, rows] + fy[s, d]
+            own[s, 0, b, rows, W] = own[s, 0, b, rows, W] + fy[s, d, :, W]
         for d in range(2):
             ny_copy(j, d).start()
         for d in range(2):
             nx_copy(j, d).wait_recv()
         for yy in (1, 0):
-            own[s, yy, x, :RX] = own[s, yy, x, :RX] + nx[s, 0, yy] + nx[s, 1, yy]
+            own[s, yy, x, :RX, W] = own[s, yy, x, :RX, W] + nx[s, 0, yy, :, W] + nx[s, 1, yy, :, W]
         yex_copy(j).start()
 
     def stage4(j):
-        s = s4(j)
+        s, W = s4(j), slice(0, width(j))
         for d in range(2):
             ny_copy(j, d).wait_recv()
-        lo = own[s, 0, x, RX:] + ny[s, 0] + ny[s, 1]
-        hid_v[RX:, cols(j, cd)] = (hid_v[RX:, cols(j, cd)].astype(F32) + lo).astype(BF16)
+        lo = own[s, 0, x, RX:, W] + ny[s, 0, :, W] + ny[s, 1, :, W]
+        hid_v[RX:, dcols(j)] = (hid_v[RX:, dcols(j)].astype(F32) + lo).astype(BF16)
         yex_copy(j).wait_recv()
-        hi = own[s, 0, x, :RX] + yex[s]
-        hid_v[:RX, cols(j, cd)] = (hid_v[:RX, cols(j, cd)].astype(F32) + hi).astype(BF16)
+        hi = own[s, 0, x, :RX, W] + yex[s, :, W]
+        hid_v[:RX, dcols(j)] = (hid_v[:RX, dcols(j)].astype(F32) + hi).astype(BF16)
         out_copy(j).start()
         yex_copy(j).wait_send()
         for d in range(2):
@@ -404,40 +487,36 @@
 
     fetch(0)
 
-    @pl.loop(0, N + 3)
+    @pl.loop(0, N - 1)
     def _(j):
         @pl.when(j + SLOTS < N)
         def _():
             wo_copy(j + SLOTS).start()
 
-        @pl.when(j < N)
-        def _():
+        down(j)
+        stage1(j)
+        pl.when(j >= 1)(lambda: stage2(j - 1))
+        pl.when(j >= 2)(lambda: stage3(j - 2))
+        pl.when(j >= 3)(lambda: stage4(j - 3))
+
+    for j in range(N - 1, N + 4):
+        if j <= N:
             down(j)
             stage1(j)
-
-        @pl.when(jnp.logical_and(j >= 1, j < N + 1))
-        def _():
-            stage2(j - 1)
-
-        @pl.when(jnp.logical_and(j >= 2, j < N + 2))
-        def _():
-            stage3(j - 2)
-
-        @pl.when(j >= 3)
-        def _():
-            stage4(j - 3)
+        for lag, stage in ((1, stage2), (2, stage3), (3, stage4)):
+            if j - lag <= N:
+                stage(j - lag)
 
     for yy in range(2):
         for d in range(2):
             u_fwd(yy, d).wait_send()
-            for part in range(2):
-                u_copy(yy, d, part).wait_send()
-        for i in range(8):
+            if yy == 1:
+                for part in range(2):
+                    u_copy(yy, d, part).wait_send()
+        for i in range(2 * (1 - yy), 8):
             u_sib(yy, i).wait_send()
-    for part in range(2):
-        u_pair(part).wait_send()
-    sib_copy(N - 1).wait_send()
-    for j in (N - 2, N - 1):
+    sib_copy(N).wait_send()
+    for j in (N - 1, N):
         yey_copy(j).wait_send()
         for d in range(2):
             for copy in (fx_copy, nx_copy, fy_copy):
@@ -446,6 +525,12 @@
     @pl.loop(0, N)
     def _(j):
         wo_copy(j).wait_send()
+
+    @pl.loop(0, N - 1)
+    def _(j):
+        out_copy(j).wait()
+
+    for j in (N - 1, N):
         out_copy(j).wait()
 
 
@@ -483,7 +568,7 @@
                 vm((S, 2, (R - RX) // 2, cd), F32),
                 vm((S, 2, R - RX, cd), F32),
                 vm((S, RX, cd), F32),
-                dma, dma, dma((8,)), dma((2, 2)), dma((N,)),
+                dma((2,)), dma((2,)), dma((2, 2)), dma((6,)), dma((2, 2)), dma((N + 1,)),
                 dma((6,)), dma((6,)), dma((6,)), dma((6,)), dma((6,)), dma((6,)), dma((N,)), dma((N,)),
                 dma((2,)), dma((2,)), dma((2, 2, 2)), dma((2, 2, 2)), dma((2, 2)), dma((2, 2)), dma((2, 8)), dma((2, 8)),
                 dma, dma((2,)), dma((2,)), dma((S,)), dma((2, 2)), dma((S, 2)), dma((2, 2)), dma((S, 2)),

time: 624 us -> 610 us (0.978)
  Pallas kernels: 617 us -> 606 us
    pallas_call x1, Pallas kernels: 617 us -> 606 us  [local_mlp(): pl.pallas_call(functools.partial(mlp_kernel, n_tp, n_y, N), out_shape=(ja...]
where the time goes in v3:
time: 610 us
  Pallas kernels  606 us (99%)
    pallas_call x1, Pallas kernels, local_mlp(): pl.pallas_call(functools.partial(mlp_kernel, n_tp, n_y, N), out_shape=(ja...  606 us

profile of v3, /device:TPU:97, one launch (start us, length us, event | category | flops | bytes accessed | tf_op | source)
XLA Modules:
  0.0 609.9 jit_solution(12746951255301307153)
XLA Ops:
  0.0 606.0 %mlp.1 = (bf16[256,6144]{1,0:T(8,128)(2,1)}, bf16[2,8,256,6144]{3,2,1,0:T(8,128)(2,1)}, bf16[768,6144]{1,0:T(8,128)(2,1)}) custom-call(bf16[256,6144]{1,0:T(8,128)(2,1)} %hid_ref.1, f32[1,6144]{1,0:T(1,128)} %bitcast.1, bf16[1536,3072]{1,0:T(8,128)(2,1)} %win_ref.1, bf16[768,6144]{1,0:T(8,128)(2,1)} %wout_ref.1), custom_call_target="tpu_custom_call" | custom-call | flops 154618822656 | bytes 150994944 | tf_op jit(solution)/shard_map/mlp/pallas_call | solution.py:548
  606.0 3.9 copy.6

commit v4 on v3

--- a/solution.py
+++ b/solution.py
@@ -20,7 +20,7 @@
 
 def mlp_kernel(
     n_tp, n_y, N, hid_ref, scale_ref, win_ref, wout_ref, out_ref, u_ref, gout_ref,
-    wb, h, ub, hid_v, own, sibst, sibr, yey, fx, nx, fy, ny, yex,
+    wb, h, w2b, ub, hid_v, own, sibst, sibr, yey, fx, nx, fy, ny, yex,
     hid_sem, ust_sem, ld_sem, ow_sem, w2_sem, out_sem,
     d_s, d_r, s_s, s_r, f_s, f_r, wo_s, wo_r,
     uy_s, uy_r, ux_s, ux_r, uf_s, uf_r, ub_s, ub_r,
@@ -31,7 +31,6 @@
     dk = win_ref.shape[0]
     K1 = 6
     cf, cd = sub // 3, D // N
-    F2 = 2 * sub
     n_x = n_tp // 2
     RX = split_rows(R)
     hx, hy = RX // 2, (R - RX) // 2
@@ -95,6 +94,36 @@
     def wo_copy(j):
         return remote(wout_ref.at[:, cols(j, cd)], gout_ref.at[:, cols(j, cd)], wo_s.at[j], wo_r.at[j], other)
 
+    def s2(j):
+        return lax.rem(j, 2)
+
+    def s4(j):
+        return lax.rem(j, SLOTS)
+
+    def width(j):
+        return cd // 2 if isinstance(j, int) and j >= N - 1 else cd
+
+    def dcols(j):
+        if width(j) == cd:
+            return cols(j, cd)
+        return pl.ds((N - 1) * cd + (j - N + 1) * (cd // 2), cd // 2)
+
+    def narrow(j):
+        return pl.ds(0, width(j))
+
+    def w2_loads(j):
+        lo, hi, w = pl.ds(0, sub), pl.ds(sub, sub), narrow(j)
+        return (
+            pltpu.make_async_copy(wout_ref.at[:, dcols(j)], w2b.at[s2(j), lo, w], w2_sem.at[s2(j), 0]),
+            pltpu.make_async_copy(gout_ref.at[:, dcols(j)], w2b.at[s2(j), hi, w], w2_sem.at[s2(j), 1]),
+        )
+
+    def fetch(j):
+        if not (isinstance(j, int) and j == N):
+            wo_copy(j).wait_recv()
+        for cp in w2_loads(j):
+            cp.start()
+
     barrier = pltpu.get_barrier_semaphore()
     for dev in (pair, other, *xnb, sib):
         pl.semaphore_signal(barrier, inc=1, device_id=dev, device_id_type=pl.DeviceIdType.MESH)
@@ -145,44 +174,30 @@
         ref = urows(yy, (tl, tr)[d], d)
         return remote(ref, ref, uf_s.at[yy, d], uf_r.at[yy, d], xnb[d])
 
-    SIB = ((t, 0), (t, 1), (tl, 0), (tr, 1), (tl, 1), (tr, 0), (tf, 0), (tf, 1))
+    SIB = ((t, 0), (t, 1), (tl, 0), (tr, 0), (tl, 1), (tr, 1), (tf, 0), (tf, 1))
 
     def u_sib(yy, i):
         ref = urows(yy, *SIB[i])
         return remote(uown(i) if yy == 0 and i < 2 else ref, ref, ub_s.at[yy, i], ub_r.at[yy, i], sib)
 
-    def u_start(yy):
-        for i in range(2):
-            u_copy(yy, 0, i).start()
-            u_copy(yy, 1, 1 - i).start()
-
-    def u_first(yy):
-        u_copy(yy, 0, 0).wait_recv()
-        u_fwd(yy, 0).start()
-        u_copy(yy, 1, 1).wait_recv()
-        u_fwd(yy, 1).start()
-        u_sib(yy, 2).start()
-        u_sib(yy, 3).start()
-
-    def u_second(yy):
-        u_copy(yy, 0, 1).wait_recv()
-        u_sib(yy, 4).start()
-        u_copy(yy, 1, 0).wait_recv()
-        u_sib(yy, 5).start()
-
-    def u_third(yy):
+    def u_start(yy, part):
+        for d in range(2):
+            u_copy(yy, d, part).start()
+
+    def u_near(yy, part):
+        for d in range(2):
+            u_copy(yy, d, part).wait_recv()
+            u_sib(yy, 2 + 2 * part + d).start()
+
+    def u_far(yy):
         for d in range(2):
             u_fwd(yy, d).wait_recv()
             u_sib(yy, 6 + d).start()
 
-    normalize(0)
-    u_copy(0, 0, 0).start()
-    u_pair(0).start()
-    normalize(1)
-    u_copy(0, 1, 1).start()
-    u_copy(0, 0, 1).start()
-    u_copy(0, 1, 0).start()
-    u_pair(1).start()
+    for part in range(2):
+        normalize(part)
+        u_start(0, part)
+        u_pair(part).start()
     for i in range(2):
         u_sib(0, i).start()
         u_store(i).start()
@@ -191,7 +206,9 @@
     for k in range(K1):
         own_w(k).start()
 
-    def block(i):
+    def block(q):
+        e, g = lax.div(q, 12), lax.div(q, 14)
+        i = q + 2 * lax.div(q, 6) * (1 - e) - 6 * (e - g)
         yy = lax.div(i, n_tp)
         m = lax.div(lax.rem(i, n_tp), 2)
         off = lax.div(m * (m + 1), 2)
@@ -239,23 +256,32 @@
         d_copy(k).wait_recv()
         f_recv(k).wait_recv()
 
+    def same(v):
+        return lambda idx: v
+
+    def straight(idx):
+        return idx
+
     s_event(0)
-    u_first(0)
-    u_second(0)
-    for i in range(2):
-        u_pair(i).wait_recv()
-    u_start(1)
-    for i in range(2):
-        u_sib(1, i).start()
+    u_near(0, 0)
+    u_pair(0).wait_recv()
+    u_start(1, 0)
+    u_sib(1, 0).start()
+    u_near(0, 1)
+    u_pair(1).wait_recv()
+    u_start(1, 1)
+    for d in range(2):
+        u_fwd(0, d).start()
+    u_sib(1, 1).start()
     s_event(1)
-    u_third(0)
-    for i in range(8):
+    u_near(1, 0)
+    s_event(2)
+    for i in range(6):
         u_sib(0, i).wait_recv()
     for i in range(2):
         u_sib(1, i).wait_recv()
     for k in range(K1):
         own_w(k).wait()
-
     for i in range(2):
         u_store(i).wait()
         u_pair(i).wait_send()
@@ -263,53 +289,63 @@
         for d in range(2):
             u_copy(0, d, i).wait_send()
 
-    def same(v):
-        return lambda idx: v
-
-    def straight(idx):
-        return idx
-
-    s_event(2)
+    w_ready(0)
+    up(8, straight, same(0), same(1))
     s_event(3)
-    w_ready(0)
     w_ready(1)
-    up(10, straight, same(0), same(2))
+    up(8, straight, same(1), same(2))
+    u_near(1, 1)
+    for d in range(2):
+        u_fwd(1, d).start()
     s_event(4)
     w_ready(2)
-    u_first(1)
-    up(10, straight, same(2), same(3))
+    for i in range(2, 6):
+        u_sib(1, i).wait_recv()
+
+    def first4(idx):
+        return lax.div(15 - idx, 12)
+
+    up(12, lambda idx: idx - 4 + 12 * first4(idx), lambda idx: 2 * (1 - first4(idx)), same(3))
     s_event(5)
     for j in range(SLOTS):
         wo_copy(j).start()
     w_ready(3)
-    up(10, straight, same(3), same(4))
-    u_second(1)
+    u_far(0)
+    up(12, straight, same(3), same(4))
     w_ready(4)
-    for i in range(2, 6):
-        u_sib(1, i).wait_recv()
-
-    def early(idx):
-        return lax.div(19 - idx, 16)
+    for i in range(6, 8):
+        u_sib(0, i).wait_recv()
+
+    def first2(idx):
+        return lax.div(25 - idx, 24)
+
+    def last_block(idx):
+        g = lax.div(idx, 20)
+        return idx - 2 + 14 * first2(idx) - 12 * (lax.div(idx, 14) - g) - 6 * g
 
     def last_event(idx):
-        @pl.when(idx == 4)
+        @pl.when(idx == 8)
         def _():
             w_ready(5)
 
-        @pl.when(idx == 11)
+        @pl.when(idx == 12)
         def _():
-            u_third(1)
-
-        @pl.when(idx == 17)
+            u_far(1)
+
+        @pl.when(idx == 15)
+        def _():
+            fetch(0)
+
+        @pl.when(idx == 21)
         def _():
             for i in range(6, 8):
                 u_sib(1, i).wait_recv()
 
     up(
-        20,
-        lambda idx: idx - 4 + 14 * early(idx),
-        lambda idx: (1 - early(idx)) * (4 + lax.div(idx, 14) - 5 * lax.div(idx, 18)),
-        lambda idx: K1 - early(idx),
+        24,
+        last_block,
+        lambda idx: (1 - first2(idx)) * (4 + lax.div(idx, 14)) - 5 * lax.div(idx, 22),
+        lambda idx: 5 + lax.div(idx + 16, 24),
         last_event,
     )
 
@@ -317,23 +353,6 @@
         f_copy(k).wait_send()
         d_copy(k).wait_send()
         s_copy(k).wait_send()
-
-    def s2(j):
-        return lax.rem(j, 2)
-
-    def s4(j):
-        return lax.rem(j, SLOTS)
-
-    def width(j):
-        return cd // 2 if isinstance(j, int) and j >= N - 1 else cd
-
-    def dcols(j):
-        if width(j) == cd:
-            return cols(j, cd)
-        return pl.ds((N - 1) * cd + (j - N + 1) * (cd // 2), cd // 2)
-
-    def narrow(j):
-        return pl.ds(0, width(j))
 
     def sib_copy(j):
         w = narrow(j)
@@ -381,22 +400,6 @@
     def send(copy, j, *a):
         when_static(j >= 2, lambda: copy(j - 2, *a).wait_send())
         copy(j, *a).start()
-
-    def w2_cols(j):
-        return pl.ds(pl.multiple_of(s2(j) * cd, 128), width(j))
-
-    def w2_loads(j):
-        lo, hi = pl.ds(0, sub), pl.ds(sub, sub)
-        return (
-            pltpu.make_async_copy(wout_ref.at[:, dcols(j)], wb.at[lo, w2_cols(j)], w2_sem.at[s2(j), 0]),
-            pltpu.make_async_copy(gout_ref.at[:, dcols(j)], wb.at[hi, w2_cols(j)], w2_sem.at[s2(j), 1]),
-        )
-
-    def fetch(j):
-        if not (isinstance(j, int) and j == N):
-            wo_copy(j).wait_recv()
-        for cp in w2_loads(j):
-            cp.start()
 
     def down(j):
         W = slice(0, width(j))
@@ -414,7 +417,7 @@
         def part(i, cc):
             yy, xx = lax.div(i, n_x), lax.rem(i, n_x)
             rows = pl.ds(pl.multiple_of((yy * n_tp + xx * 2 + cc) * R, 16), R)
-            return jnp.dot(h[rows, :], wb[:F2, w2_cols(j)], preferred_element_type=F32)
+            return jnp.dot(h[rows, :], w2b[s2(j), :, W], preferred_element_type=F32)
 
         @pl.loop(0, 2 * n_x)
         def _(i):
@@ -484,8 +487,6 @@
         yex_copy(j).wait_send()
         for d in range(2):
             ny_copy(j, d).wait_send()
-
-    fetch(0)
 
     @pl.loop(0, N - 1)
     def _(j):
@@ -557,6 +558,7 @@
             scratch_shapes=[
                 vm((D, 2 * sub), BF16),
                 vm((2 * n_tp * R, 2 * sub), BF16),
+                vm((2, 2 * sub, cd), BF16),
                 vm((2, R, D), BF16),
                 vm((R, D), BF16),
                 vm((S, 2, n_x, R, cd), F32),

time: 610 us -> 609 us (level)
  no operation moved by 1% of the time
where the time goes in v4:
time: 609 us
  Pallas kernels  605 us (99%)
    pallas_call x1, Pallas kernels, local_mlp(): pl.pallas_call(functools.partial(mlp_kernel, n_tp, n_y, N), out_shape=(ja...  605 us

profile of v4, /device:TPU:97, one launch (start us, length us, event | category | flops | bytes accessed | tf_op | source)
XLA Modules:
  0.0 608.7 jit_solution(15443219577236040264)
XLA Ops:
  0.0 604.8 %mlp.1 = (bf16[256,6144]{1,0:T(8,128)(2,1)}, bf16[2,8,256,6144]{3,2,1,0:T(8,128)(2,1)}, bf16[768,6144]{1,0:T(8,128)(2,1)}) custom-call(bf16[256,6144]{1,0:T(8,128)(2,1)} %hid_ref.1, f32[1,6144]{1,0:T(1,128)} %bitcast.1, bf16[1536,3072]{1,0:T(8,128)(2,1)} %win_ref.1, bf16[768,6144]{1,0:T(8,128)(2,1)} %wout_ref.1), custom_call_target="tpu_custom_call" | custom-call | flops 154618822656 | bytes 150994944 | tf_op jit(solution)/shard_map/mlp/pallas_call | solution.py:549
  604.8 3.9 copy.6

commit v5 on v4

--- a/solution.py
+++ b/solution.py
@@ -69,27 +69,27 @@
 
     def own_w(k):
         return pltpu.make_async_copy(
-            win_ref.at[:, win_cols(y, yd, k)], wb.at[wrows(y), cols(k, cf)], ow_sem.at[k]
+            win_ref.at[:, win_cols(y, yd, k)], wb.at[k, wrows(y)], ow_sem.at[k]
         )
 
     def d_copy(k):
         return remote(
-            win_ref.at[:, win_cols(yd, y, k)], wb.at[wrows(y), cols(k, cf)], d_s.at[k], d_r.at[k], other
+            win_ref.at[:, win_cols(yd, y, k)], wb.at[k, wrows(y)], d_s.at[k], d_r.at[k], other
         )
 
     def s_copy(k):
         return remote(
-            win_ref.at[:, win_cols(yp, yo, k)], wb.at[wrows(y), cols(k, cf)], s_s.at[k], s_r.at[k], pair
+            win_ref.at[:, win_cols(yp, yo, k)], wb.at[k, wrows(y)], s_s.at[k], s_r.at[k], pair
         )
 
     def f_copy(k):
         kk = lax.rem(k + 3, K1)
         return remote(
-            wb.at[wrows(yp), cols(k, cf)], wb.at[wrows(yp), cols(kk, cf)], f_s.at[kk], f_r.at[kk], other
+            wb.at[k, wrows(yp)], wb.at[kk, wrows(yp)], f_s.at[kk], f_r.at[kk], other
         )
 
     def f_recv(k):
-        return remote(wb.at[wrows(yo), cols(k, cf)], wb.at[wrows(yo), cols(k, cf)], f_s.at[k], f_r.at[k], other)
+        return remote(wb.at[k, wrows(yo)], wb.at[k, wrows(yo)], f_s.at[k], f_r.at[k], other)
 
     def wo_copy(j):
         return remote(wout_ref.at[:, cols(j, cd)], gout_ref.at[:, cols(j, cd)], wo_s.at[j], wo_r.at[j], other)
@@ -142,6 +142,7 @@
 
     TR = 16
     hr = R // 2
+    lr = max(R // 4, 16)
 
     def normalize(part):
         hid_load(part).wait()
@@ -219,8 +220,10 @@
             yy, tt = block(blk(idx))
             s = lax.rem(idx, 2)
             return [
-                pltpu.make_async_copy(urows(yy, tt, p), ub.at[s, pl.ds(p * hr, hr), :], ld_sem.at[s, p])
-                for p in range(2)
+                pltpu.make_async_copy(
+                    u_ref.at[yy, tt, pl.ds(p * lr, lr), :], ub.at[s, pl.ds(p * lr, lr), :], ld_sem.at[s, p]
+                )
+                for p in range(R // lr)
             ]
 
         for cp in loads(0):
@@ -244,7 +247,7 @@
             @pl.loop(m0(idx), m1(idx))
             def _(m):
                 k = kseq(m)
-                pre = jnp.dot(ub[lax.rem(idx, 2)], wb[:, cols(k, cf)], preferred_element_type=F32)
+                pre = jnp.dot(ub[lax.rem(idx, 2)], wb[k], preferred_element_type=F32)
                 h[rows, cols(k, cf)] = jax.nn.gelu(pre, approximate=True).astype(BF16)
 
     def s_event(m):
@@ -289,65 +292,67 @@
         for d in range(2):
             u_copy(0, d, i).wait_send()
 
+    s_event(3)
     w_ready(0)
-    up(8, straight, same(0), same(1))
-    s_event(3)
     w_ready(1)
-    up(8, straight, same(1), same(2))
-    u_near(1, 1)
-    for d in range(2):
-        u_fwd(1, d).start()
+
+    def event1(idx):
+        @pl.when(idx == 3)
+        def _():
+            u_near(1, 1)
+            for d in range(2):
+                u_fwd(1, d).start()
+
+    up(8, straight, same(0), same(2), event1)
     s_event(4)
     w_ready(2)
     for i in range(2, 6):
         u_sib(1, i).wait_recv()
-
-    def first4(idx):
-        return lax.div(15 - idx, 12)
-
-    up(12, lambda idx: idx - 4 + 12 * first4(idx), lambda idx: 2 * (1 - first4(idx)), same(3))
+    up(4, lambda idx: idx + 8, same(0), same(3))
     s_event(5)
     for j in range(SLOTS):
         wo_copy(j).start()
     w_ready(3)
-    u_far(0)
-    up(12, straight, same(3), same(4))
+
+    def event2(idx):
+        @pl.when(idx == 3)
+        def _():
+            u_far(0)
+
+    up(8, straight, same(2), same(4), event2)
     w_ready(4)
-    for i in range(6, 8):
-        u_sib(0, i).wait_recv()
-
-    def first2(idx):
-        return lax.div(25 - idx, 24)
-
-    def last_block(idx):
-        g = lax.div(idx, 20)
-        return idx - 2 + 14 * first2(idx) - 12 * (lax.div(idx, 14) - g) - 6 * g
+
+    def first6(idx):
+        return lax.div(21 - idx, 16)
+
+    def last_m0(idx):
+        e = first6(idx)
+        return e * (3 - 3 * lax.div(idx + 18, 22)) + (1 - e) * (4 + lax.div(idx, 14) - 5 * lax.div(idx, 20))
 
     def last_event(idx):
-        @pl.when(idx == 8)
+        @pl.when(idx == 3)
+        def _():
+            for i in range(6, 8):
+                u_sib(0, i).wait_recv()
+
+        @pl.when(idx == 6)
         def _():
             w_ready(5)
 
-        @pl.when(idx == 12)
+        @pl.when(idx == 10)
         def _():
             u_far(1)
 
-        @pl.when(idx == 15)
+        @pl.when(idx == 14)
         def _():
             fetch(0)
 
-        @pl.when(idx == 21)
+        @pl.when(idx == 19)
         def _():
             for i in range(6, 8):
                 u_sib(1, i).wait_recv()
 
-    up(
-        24,
-        last_block,
-        lambda idx: (1 - first2(idx)) * (4 + lax.div(idx, 14)) - 5 * lax.div(idx, 22),
-        lambda idx: 5 + lax.div(idx + 16, 24),
-        last_event,
-    )
+    up(22, lambda idx: idx - 6 + 14 * first6(idx), last_m0, lambda idx: K1 - first6(idx), last_event)
 
     for k in range(K1):
         f_copy(k).wait_send()
@@ -556,7 +561,7 @@
             in_specs=[any_spec, pl.BlockSpec(memory_space=vm), any_spec, any_spec],
             out_specs=(any_spec, any_spec, any_spec),
             scratch_shapes=[
-                vm((D, 2 * sub), BF16),
+                vm((6, D, sub // 3), BF16),
                 vm((2 * n_tp * R, 2 * sub), BF16),
                 vm((2, 2 * sub, cd), BF16),
                 vm((2, R, D), BF16),
@@ -570,7 +575,7 @@
                 vm((S, 2, (R - RX) // 2, cd), F32),
                 vm((S, 2, R - RX, cd), F32),
                 vm((S, RX, cd), F32),
-                dma((2,)), dma((2,)), dma((2, 2)), dma((6,)), dma((2, 2)), dma((N + 1,)),
+                dma((2,)), dma((2,)), dma((2, 4)), dma((6,)), dma((2, 2)), dma((N + 1,)),
                 dma((6,)), dma((6,)), dma((6,)), dma((6,)), dma((6,)), dma((6,)), dma((N,)), dma((N,)),
                 dma((2,)), dma((2,)), dma((2, 2, 2)), dma((2, 2, 2)), dma((2, 2)), dma((2, 2)), dma((2, 8)), dma((2, 8)),
                 dma, dma((2,)), dma((2,)), dma((S,)), dma((2, 2)), dma((S, 2)), dma((2, 2)), dma((S, 2)),

time: 609 us -> 595 us (0.977)
  Pallas kernels: 605 us -> 590 us
    pallas_call x1, Pallas kernels: 605 us -> 590 us  [local_mlp(): pl.pallas_call(functools.partial(mlp_kernel, n_tp, n_y, N), out_shape=(ja...]
where the time goes in v5:
time: 595 us; the launch traced here: 594 us
  Pallas kernels  590 us (99%)
    pallas_call x1, Pallas kernels, local_mlp(): pl.pallas_call(functools.partial(mlp_kernel, n_tp, n_y, N), out_shape=(ja...  590 us

profile of v5, /device:TPU:97, one launch (start us, length us, event | category | flops | bytes accessed | tf_op | source)
XLA Modules:
  0.0 593.5 jit_solution(16405550547210820205)
XLA Ops:
  0.0 589.6 %mlp.1 = (bf16[256,6144]{1,0:T(8,128)(2,1)}, bf16[2,8,256,6144]{3,2,1,0:T(8,128)(2,1)}, bf16[768,6144]{1,0:T(8,128)(2,1)}) custom-call(bf16[256,6144]{1,0:T(8,128)(2,1)} %hid_ref.1, f32[1,6144]{1,0:T(1,128)} %bitcast.1, bf16[1536,3072]{1,0:T(8,128)(2,1)} %win_ref.1, bf16[768,6144]{1,0:T(8,128)(2,1)} %wout_ref.1), custom_call_target="tpu_custom_call" | custom-call | flops 154618822656 | bytes 150994944 | tf_op jit(solution)/shard_map/mlp/pallas_call | solution.py:554
  589.6 3.9 copy.6

commit v6 on v0

v6 whole, which is shorter than its diff:
```python
import functools

import jax
import jax.numpy as jnp
from jax import lax
from jax.experimental import pallas as pl
from jax.experimental.pallas import tpu as pltpu
from jax.sharding import PartitionSpec as P

LN_EPS = 1e-6
CHUNKS = 24
F32 = jnp.float32
BF16 = jnp.bfloat16
SLOTS = 4
NB = 5


def split_rows(R):
    return R * 9 // 16 // 16 * 16


def mlp_kernel(
    n_tp, n_y, N, hid_ref, scale_ref, win_ref, wout_ref, out_ref, u_ref, gout_ref,
    wb, h, w2b, hid_v, sibr, yey, fx, nx, fy, ny, yex,
    hid_sem, ust_sem, ld_sem, ow_sem, w2_sem, out_sem,
    d_s, d_r, s_s, s_r, f_s, f_r, wo_s, wo_r,
    uy_s, uy_r, ux_s, ux_r, uf_s, uf_r, ub_s, ub_r,
    sb_s, sb_r, yey_s, yey_r, fx_s, fx_r, nx_s, nx_r, fy_s, fy_r, ny_s, ny_r, yex_s, yex_r,
):
    R, D = hid_v.shape
    sub = wout_ref.shape[0]
    dk = win_ref.shape[0]
    K1 = 6
    cf, cd = sub // 3, D // N
    n_x = n_tp // 2
    RX = split_rows(R)
    hx, hy = RX // 2, (R - RX) // 2
    t = lax.axis_index("tp")
    y = lax.axis_index("fsdp")
    x, c = lax.div(t, 2), lax.rem(t, 2)
    xr, xl, xf = lax.rem(x + 1, n_x), lax.rem(x + n_x - 1, n_x), lax.rem(x + 2, n_x)
    tr, tl, tf = xr * 2 + c, xl * 2 + c, xf * 2 + c
    tsib = x * 2 + 1 - c
    yp = lax.div(y, 2) * 2 + 1 - lax.rem(y, 2)
    yd = n_y - 1 - y
    yo = n_y - 1 - yp
    pair, other, sib = {"fsdp": yp}, {"fsdp": yd}, {"tp": tsib}
    xnb = ({"tp": tr}, {"tp": tl})

    def remote(src, dst, s, r, dev):
        return pltpu.make_async_remote_copy(
            src_ref=src, dst_ref=dst, send_sem=s, recv_sem=r, device_id=dev, device_id_type=pl.DeviceIdType.MESH
        )

    def cols(k, n):
        return pl.ds(pl.multiple_of(k * n, 128), n)

    def wrows(o):
        return pl.ds(pl.multiple_of(o * dk, 16), dk)

    def sseq(m):
        return lax.rem(m, 2) * 3 + lax.div(m, 2)

    def kseq(m):
        return lax.rem(m + 1, 2) * 3 + lax.div(m, 2)

    def win_cols(first, second, k):
        s = jnp.where(k < 3, first, second) if not isinstance(k, int) else (first if k < 3 else second)
        return pl.ds(pl.multiple_of(s * sub + lax.rem(k, 3) * cf, 128), cf)

    def own_w(k):
        return pltpu.make_async_copy(
            win_ref.at[:, win_cols(y, yd, k)], wb.at[k, wrows(y)], ow_sem.at[k]
        )

    def d_copy(k):
        return remote(
            win_ref.at[:, win_cols(yd, y, k)], wb.at[k, wrows(y)], d_s.at[k], d_r.at[k], other
        )

    def s_copy(k):
        return remote(
            win_ref.at[:, win_cols(yp, yo, k)], wb.at[k, wrows(y)], s_s.at[k], s_r.at[k], pair
        )

    def f_copy(k):
        kk = lax.rem(k + 3, K1)
        return remote(
            wb.at[k, wrows(yp)], wb.at[kk, wrows(yp)], f_s.at[kk], f_r.at[kk], other
        )

    def f_recv(k):
        return remote(wb.at[k, wrows(yo)], wb.at[k, wrows(yo)], f_s.at[k], f_r.at[k], other)

    def wo_copy(j):
        return remote(wout_ref.at[:, cols(j, cd)], gout_ref.at[:, cols(j, cd)], wo_s.at[j], wo_r.at[j], other)

    def s2(j):
        return lax.rem(j, 2)

    def s4(j):
        return lax.rem(j, SLOTS)

    def width(j):
        return cd // 2 if isinstance(j, int) and j >= N - 1 else cd

    def dcols(j):
        if width(j) == cd:
            return cols(j, cd)
        return pl.ds((N - 1) * cd + (j - N + 1) * (cd // 2), cd // 2)

    def narrow(j):
        return pl.ds(0, width(j))

    def w2_loads(j):
        lo, hi, w = pl.ds(0, sub), pl.ds(sub, sub), narrow(j)
        return (
            pltpu.make_async_copy(wout_ref.at[:, dcols(j)], w2b.at[s2(j), lo, w], w2_sem.at[s2(j), 0]),
            pltpu.make_async_copy(gout_ref.at[:, dcols(j)], w2b.at[s2(j), hi, w], w2_sem.at[s2(j), 1]),
        )

    def fetch(j):
        if not (isinstance(j, int) and j == N):
            wo_copy(j).wait_recv()
        for cp in w2_loads(j):
            cp.start()

    barrier = pltpu.get_barrier_semaphore()
    for dev in (pair, other, *xnb, sib):
        pl.semaphore_signal(barrier, inc=1, device_id=dev, device_id_type=pl.DeviceIdType.MESH)

    def hid_load(part):
        rows = pl.ds(part * (R // 2), R // 2)
        return pltpu.make_async_copy(hid_ref.at[rows], hid_v.at[rows], hid_sem.at[part])

    for part in range(2):
        hid_load(part).start()
    pl.semaphore_wait(barrier, 5)

    for m in range(2):
        s_copy((m % 2) * 3 + m // 2).start()
        d_copy(((m + 1) % 2) * 3 + m // 2).start()

    def phase1(ub):
        TR = 16
        hr = R // 2
        lr = max(R // 4, 16)

        def normalize(part):
            hid_load(part).wait()

            @pl.loop(0, hr // TR)
            def _(i):
                rows = pl.ds(pl.multiple_of(part * hr + i * TR, TR), TR)
                v = hid_v[rows, :].astype(F32)
                cen = v - jnp.mean(v, axis=-1, keepdims=True)
                var = jnp.mean(cen * cen, axis=-1, keepdims=True)
                ub[0, rows, :] = (cen * lax.rsqrt(var + LN_EPS) * scale_ref[...]).astype(BF16)

        def urows(yy, tt, part):
            return u_ref.at[yy, tt, pl.ds(part * hr, hr), :]

        def uown(part):
            return ub.at[0, pl.ds(part * hr, hr), :]

        def u_store(part):
            return pltpu.make_async_copy(uown(part), urows(0, t, part), ust_sem.at[part])

        def u_pair(part):
            return remote(uown(part), urows(1, t, part), uy_s.at[part], uy_r.at[part], pair)

        def u_copy(yy, d, part):
            ref = urows(yy, t, part)
            return remote(uown(part) if yy == 0 else ref, ref, ux_s.at[yy, d, part], ux_r.at[yy, d, part], xnb[d])

        def u_fwd(yy, d):
            ref = urows(yy, (tl, tr)[d], d)
            return remote(ref, ref, uf_s.at[yy, d], uf_r.at[yy, d], xnb[d])

        SIB = ((t, 0), (t, 1), (tl, 0), (tr, 0), (tl, 1), (tr, 1), (tf, 0), (tf, 1))

        def u_sib(yy, i):
            ref = urows(yy, *SIB[i])
            return remote(uown(i) if yy == 0 and i < 2 else ref, ref, ub_s.at[yy, i], ub_r.at[yy, i], sib)

        def u_start(yy, part):
            for d in range(2):
                u_copy(yy, d, part).start()

        def u_near(yy, part):
            for d in range(2):
                u_copy(yy, d, part).wait_recv()
                u_sib(yy, 2 + 2 * part + d).start()

        def u_far(yy):
            for d in range(2):
                u_fwd(yy, d).wait_recv()
                u_sib(yy, 6 + d).start()

        for part in range(2):
            normalize(part)
            u_start(0, part)
            u_pair(part).start()
        for i in range(2):
            u_sib(0, i).start()
            u_store(i).start()
        for m in range(2, K1):
            s_copy((m % 2) * 3 + m // 2).start()
        for k in range(K1):
            own_w(k).start()

        def block(q):
            e, g = lax.div(q, 12), lax.div(q, 14)
            i = q + 2 * lax.div(q, 6) * (1 - e) - 6 * (e - g)
            yy = lax.div(i, n_tp)
            m = lax.div(lax.rem(i, n_tp), 2)
            off = lax.div(m * (m + 1), 2)
            return yy, lax.rem(x + off, n_x) * 2 + lax.rem(i, 2)

        def up(n, blk, m0, m1, event=None):
            def loads(idx):
                yy, tt = block(blk(idx))
                s = lax.rem(idx, NB)
                return [
                    pltpu.make_async_copy(
                        u_ref.at[yy, tt, pl.ds(p * lr, lr), :], ub.at[s, pl.ds(p * lr, lr), :], ld_sem.at[s, p]
                    )
                    for p in range(R // lr)
                ]

            for i in range(min(NB - 1, n)):
                for cp in loads(i):
                    cp.start()

            @pl.loop(0, n)
            def _(idx):
                if event is not None:
                    event(idx)

                @pl.when(idx + NB - 1 < n)
                def _():
                    for cp in loads(idx + NB - 1):
                        cp.start()

                for cp in loads(idx):
                    cp.wait()
                yy, tt = block(blk(idx))
                rows = pl.ds(pl.multiple_of((yy * n_tp + tt) * R, 16), R)

                @pl.loop(m0(idx), m1(idx))
                def _(m):
                    k = kseq(m)
                    pre = jnp.dot(ub[lax.rem(idx, NB)], wb[k], preferred_element_type=F32)
                    h[rows, cols(k, cf)] = jax.nn.gelu(pre, approximate=True).astype(BF16)

        def s_event(m):
            s_copy(sseq(m)).wait_recv()
            f_copy(sseq(m)).start()

        def w_ready(m):
            k = kseq(m)
            d_copy(k).wait_recv()
            f_recv(k).wait_recv()

        def same(v):
            return lambda idx: v

        def straight(idx):
            return idx

        s_event(0)
        s_event(1)
        for m in range(2, K1):
            d_copy(((m + 1) % 2) * 3 + m // 2).start()
        u_near(0, 0)
        u_pair(0).wait_recv()
        u_start(1, 0)
        u_sib(1, 0).start()
        u_near(0, 1)
        u_pair(1).wait_recv()
        u_start(1, 1)
        for d in range(2):
            u_fwd(0, d).start()
        u_sib(1, 1).start()
        u_near(1, 0)
        for i in range(6):
            u_sib(0, i).wait_recv()
        for i in range(2):
            u_sib(1, i).wait_recv()
        for k in range(K1):
            own_w(k).wait()
        for i in range(2):
            u_store(i).wait()
            u_pair(i).wait_send()
            u_sib(0, i).wait_send()
            for d in range(2):
                u_copy(0, d, i).wait_send()

        w_ready(0)
        w_ready(1)

        def event1(idx):
            @pl.when(idx == 5)
            def _():
                s_event(2)

        up(8, straight, same(0), same(2), event1)
        s_event(3)
        u_near(1, 1)
        for d in range(2):
            u_fwd(1, d).start()
        for i in range(2, 6):
            u_sib(1, i).wait_recv()
        up(4, lambda idx: idx + 8, same(0), same(2))
        s_event(4)
        w_ready(2)
        up(12, straight, same(2), same(3))
        s_event(5)
        for j in range(SLOTS):
            wo_copy(j).start()
        w_ready(3)

        def event2(idx):
            @pl.when(idx == 5)
            def _():
                u_far(0)

        up(12, straight, same(3), same(4), event2)
        w_ready(4)
        for i in range(6, 8):
            u_sib(0, i).wait_recv()

        def first2(idx):
            return lax.div(25 - idx, 24)

        def last_block(idx):
            g = lax.div(idx, 20)
            return idx - 2 + 14 * first2(idx) - 12 * (lax.div(idx, 14) - g) - 6 * g

        def last_event(idx):
            @pl.when(idx == 8)
            def _():
                w_ready(5)

            @pl.when(idx == 12)
            def _():
                u_far(1)

            @pl.when(idx == 15)
            def _():
                fetch(0)

            @pl.when(idx == 18)
            def _():
                for i in range(6, 8):
                    u_sib(1, i).wait_recv()

        up(
            24,
            last_block,
            lambda idx: (1 - first2(idx)) * (4 + lax.div(idx, 14)) - 5 * lax.div(idx, 22),
            lambda idx: 5 + lax.div(idx + 16, 24),
            last_event,
        )

        for yy in range(2):
            for d in range(2):
                u_fwd(yy, d).wait_send()
                if yy == 1:
                    for part in range(2):
                        u_copy(yy, d, part).wait_send()
            for i in range(2 * (1 - yy), 8):
                u_sib(yy, i).wait_send()

    pl.run_scoped(phase1, pltpu.VMEM((NB, R, D), BF16))

    for k in range(K1):
        f_copy(k).wait_send()
        d_copy(k).wait_send()
        s_copy(k).wait_send()

    def phase2(own, sibst):
        def sib_copy(j):
            w = narrow(j)
            return remote(sibst.at[:, :, :, w], sibr.at[s2(j), :, :, :, w], sb_s, sb_r.at[s2(j)], sib)

        def yey_copy(j):
            w = narrow(j)
            src = own.at[s4(j), 1, :, pl.ds(RX, R - RX), w]
            return remote(src, yey.at[s4(j), :, :, w], yey_s.at[s2(j)], yey_r.at[s4(j)], pair)

        def yex_copy(j):
            w = narrow(j)
            return remote(own.at[s4(j), 1, x, pl.ds(0, RX), w], yex.at[s4(j), :, w], yex_s.at[s2(j)], yex_r.at[s4(j)], pair)

        def fx_copy(j, d):
            w = narrow(j)
            src = own.at[s4(j), :, xf, pl.ds(d * hx, hx), w]
            return remote(src, fx.at[s4(j), d, :, :, w], fx_s.at[s2(j), d], fx_r.at[s4(j), d], xnb[d])

        def nx_copy(j, d):
            w = narrow(j)
            src = own.at[s4(j), :, (xr, xl)[d], pl.ds(0, RX), w]
            return remote(src, nx.at[s4(j), d, :, :, w], nx_s.at[s2(j), d], nx_r.at[s4(j), d], xnb[d])

        def fy_copy(j, d):
            w = narrow(j)
            src = own.at[s4(j), 0, xf, pl.ds(RX + d * hy, hy), w]
            return remote(src, fy.at[s4(j), d, :, w], fy_s.at[s2(j), d], fy_r.at[s4(j), d], xnb[d])

        def ny_copy(j, d):
            w = narrow(j)
            src = own.at[s4(j), 0, (xr, xl)[d], pl.ds(RX, R - RX), w]
            return remote(src, ny.at[s4(j), d, :, w], ny_s.at[s2(j), d], ny_r.at[s4(j), d], xnb[d])

        def out_copy(j):
            return pltpu.make_async_copy(hid_v.at[:, dcols(j)], out_ref.at[:, dcols(j)], out_sem.at[j])

        def when_static(cond, fn):
            if isinstance(cond, bool):
                if cond:
                    fn()
            else:
                pl.when(cond)(fn)

        def send(copy, j, *a):
            when_static(j >= 2, lambda: copy(j - 2, *a).wait_send())
            copy(j, *a).start()

        def down(j):
            W = slice(0, width(j))
            for cp in w2_loads(j):
                cp.wait()

            if isinstance(j, int):
                if j < N:
                    fetch(j + 1)
            else:
                pl.when(j + 1 < N - 1)(lambda: fetch(j + 1))
                pl.when(j + 1 == N - 1)(lambda: fetch(N - 1))
            when_static(j >= 1, lambda: sib_copy(j - 1).wait_send())

            def part(i, cc):
                yy, xx = lax.div(i, n_x), lax.rem(i, n_x)
                rows = pl.ds(pl.multiple_of((yy * n_tp + xx * 2 + cc) * R, 16), R)
                return jnp.dot(h[rows, :], w2b[s2(j), :, W], preferred_element_type=F32)

            @pl.loop(0, 2 * n_x)
            def _(i):
                sibst[lax.div(i, n_x), lax.rem(i, n_x), :, W] = part(i, 1 - c)

            sib_copy(j).start()

            @pl.loop(0, 2 * n_x)
            def _(i):
                own[s4(j), lax.div(i, n_x), lax.rem(i, n_x), :, W] = part(i, c)

        def stage1(j):
            W = slice(0, width(j))
            sib_copy(j).wait_recv()

            @pl.loop(0, 2 * n_x)
            def _(i):
                yy, xx = lax.div(i, n_x), lax.rem(i, n_x)
                own[s4(j), yy, xx, :, W] = own[s4(j), yy, xx, :, W] + sibr[s2(j), yy, xx, :, W]

            send(yey_copy, j)
            for d in range(2):
                send(fx_copy, j, d)

        def stage2(j):
            s, W = s4(j), slice(0, width(j))
            for d in range(2):
                fx_copy(j, d).wait_recv()
                b, rows = (xr, xl)[d], slice(d * hx, (d + 1) * hx)
                for yy in range(2):
                    own[s, yy, b, rows, W] = own[s, yy, b, rows, W] + fx[s, d, yy, :, W]
            for d in range(2):
                send(nx_copy, j, d)
            yey_copy(j).wait_recv()

            @pl.loop(0, n_x)
            def _(i):
                own[s, 0, i, RX:, W] = own[s, 0, i, RX:, W] + yey[s, i, :, W]

            for d in range(2):
                send(fy_copy, j, d)

        def stage3(j):
            s, W = s4(j), slice(0, width(j))
            for d in range(2):
                fy_copy(j, d).wait_recv()
                b, rows = (xr, xl)[d], slice(RX + d * hy, RX + (d + 1) * hy)
                own[s, 0, b, rows, W] = own[s, 0, b, rows, W] + fy[s, d, :, W]
            for d in range(2):
                ny_copy(j, d).start()
            for d in range(2):
                nx_copy(j, d).wait_recv()
            for yy in (1, 0):
                own[s, yy, x, :RX, W] = own[s, yy, x, :RX, W] + nx[s, 0, yy, :, W] + nx[s, 1, yy, :, W]
            yex_copy(j).start()

        def stage4(j):
            s, W = s4(j), slice(0, width(j))
            for d in range(2):
                ny_copy(j, d).wait_recv()
            lo = own[s, 0, x, RX:, W] + ny[s, 0, :, W] + ny[s, 1, :, W]
            hid_v[RX:, dcols(j)] = (hid_v[RX:, dcols(j)].astype(F32) + lo).astype(BF16)
            yex_copy(j).wait_recv()
            hi = own[s, 0, x, :RX, W] + yex[s, :, W]
            hid_v[:RX, dcols(j)] = (hid_v[:RX, dcols(j)].astype(F32) + hi).astype(BF16)
            out_copy(j).start()
            yex_copy(j).wait_send()
            for d in range(2):
                ny_copy(j, d).wait_send()

        @pl.loop(0, N - 1)
        def _(j):
            @pl.when(j + SLOTS < N)
            def _():
                wo_copy(j + SLOTS).start()

            down(j)
            stage1(j)
            pl.when(j >= 1)(lambda: stage2(j - 1))
            pl.when(j >= 2)(lambda: stage3(j - 2))
            pl.when(j >= 3)(lambda: stage4(j - 3))

        for j in range(N - 1, N + 4):
            if j <= N:
                down(j)
                stage1(j)
            for lag, stage in ((1, stage2), (2, stage3), (3, stage4)):
                if j - lag <= N:
                    stage(j - lag)

        sib_copy(N).wait_send()
        for j in (N - 1, N):
            yey_copy(j).wait_send()
            for d in range(2):
                for copy in (fx_copy, nx_copy, fy_copy):
                    copy(j, d).wait_send()

        @pl.loop(0, N)
        def _(j):
            wo_copy(j).wait_send()

        @pl.loop(0, N - 1)
        def _(j):
            out_copy(j).wait()

        for j in (N - 1, N):
            out_copy(j).wait()

    pl.run_scoped(phase2, pltpu.VMEM((SLOTS, 2, n_x, R, cd), F32), pltpu.VMEM((2, n_x, R, cd), F32))


def make_local(n_tp, n_y, N):
    def local_mlp(hidden, ln_scale, w_in, w_out):
        R, D = hidden.shape
        sub = w_out.shape[0]
        cd = D // N
        n_x = n_tp // 2
        RX = split_rows(R)
        any_spec = pl.BlockSpec(memory_space=pl.ANY)
        dma = pltpu.SemaphoreType.DMA
        vm = pltpu.VMEM
        S = SLOTS
        out, _, _ = pl.pallas_call(
            functools.partial(mlp_kernel, n_tp, n_y, N),
            out_shape=(
                jax.ShapeDtypeStruct((R, D), BF16),
                jax.ShapeDtypeStruct((2, n_tp, R, D), BF16),
                jax.ShapeDtypeStruct((sub, D), BF16),
            ),
            in_specs=[any_spec, pl.BlockSpec(memory_space=vm), any_spec, any_spec],
            out_specs=(any_spec, any_spec, any_spec),
            scratch_shapes=[
                vm((6, D, sub // 3), BF16),
                vm((2 * n_tp * R, 2 * sub), BF16),
                vm((2, 2 * sub, cd), BF16),
                vm((R, D), BF16),
                vm((2, 2, n_x, R, cd), F32),
                vm((S, n_x, R - RX, cd), F32),
                vm((S, 2, 2, RX // 2, cd), F32),
                vm((S, 2, 2, RX, cd), F32),
                vm((S, 2, (R - RX) // 2, cd), F32),
                vm((S, 2, R - RX, cd), F32),
                vm((S, RX, cd), F32),
                dma((2,)), dma((2,)), dma((NB, 4)), dma((6,)), dma((2, 2)), dma((N + 1,)),
                dma((6,)), dma((6,)), dma((6,)), dma((6,)), dma((6,)), dma((6,)), dma((N,)), dma((N,)),
                dma((2,)), dma((2,)), dma((2, 2, 2)), dma((2, 2, 2)), dma((2, 2)), dma((2, 2)), dma((2, 8)), dma((2, 8)),
                dma, dma((2,)), dma((2,)), dma((S,)), dma((2, 2)), dma((S, 2)), dma((2, 2)), dma((S, 2)),
                dma((2, 2)), dma((S, 2)), dma((2, 2)), dma((S, 2)), dma((2,)), dma((S,)),
            ],
            compiler_params=pltpu.CompilerParams(
                collective_id=0, has_side_effects=True, vmem_limit_bytes=67043328
            ),
            cost_estimate=pl.CostEstimate(
                flops=4 * n_tp * R * D * w_in.shape[1], bytes_accessed=8 * D * w_in.shape[1], transcendentals=0
            ),
            name="mlp",
        )(hidden, ln_scale.reshape(1, D), w_in, w_out)
        return out

    return local_mlp


def solution(mesh):
    return jax.shard_map(
        make_local(mesh.shape["tp"], mesh.shape["fsdp"], CHUNKS),
        mesh=mesh,
        in_specs=(P(("data", "fsdp", "tp"), None), P(None), P("fsdp", "tp"), P(("tp", "fsdp"), None)),
        out_specs=P(("data", "fsdp", "tp"), None),
        check_vma=False,
    )
```

time: 1150 us -> 588 us (0.51)
  waiting for transfers between devices: 940 us -> 0 us
  Pallas kernels: 0 us -> 583 us
  matrix products: 183 us -> 0 us
  other arithmetic: 15.4 us -> 0 us
  between operations: 13.2 us -> 0.01 us
    all_gather x3 -> x0, waiting for transfers between devices: 691 us -> none  [the longest x1 329 us: local_mlp(): w_in_tp = lax.all_gather(w_in, 'fsdp', axis=0, tiled=True)]
    pallas_call x0 -> x1, Pallas kernels: none -> 583 us  [local_mlp(): pl.pallas_call(functools.partial(mlp_kernel, n_tp, n_y, N), out_shape=(ja...]
    reduce_scatter x1 -> x0, waiting for transfers between devices: 247 us -> none  [local_mlp(): mlp_out = lax.psum_scatter(part_sum, 'tp', scatter_dimension=0, tiled=True)]
    dot_general x2 -> x0, matrix products: 183 us -> none  [the longest x1 95.1 us: local_mlp(): part_sum = jnp.dot(act_out, w_out_tp, preferred_element_type=jnp.float32)]
  transfers between devices with their start and end apart: 4 -> 0, of which waited for: 4 -> 0; matrix products, arithmetic and copies ran while one was open for 8% -> 0% of each run, Pallas kernels for 0% -> 0%
where the time goes in v6:
time: 588 us; the launch traced here: 587 us
  Pallas kernels  583 us (99%)
    pallas_call x1, Pallas kernels, local_mlp(): pl.pallas_call(functools.partial(mlp_kernel, n_tp, n_y, N), out_shape=(ja...  583 us

profile of v6, /device:TPU:97, one launch (start us, length us, event | category | flops | bytes accessed | tf_op | source)
XLA Modules:
  0.0 586.9 jit_solution(3510843268852468372)
XLA Ops:
  0.0 583.0 %mlp.1 = (bf16[256,6144]{1,0:T(8,128)(2,1)}, bf16[2,8,256,6144]{3,2,1,0:T(8,128)(2,1)}, bf16[768,6144]{1,0:T(8,128)(2,1)}) custom-call(bf16[256,6144]{1,0:T(8,128)(2,1)} %hid_ref.1, f32[1,6144]{1,0:T(1,128)} %bitcast.1, bf16[1536,3072]{1,0:T(8,128)(2,1)} %win_ref.1, bf16[768,6144]{1,0:T(8,128)(2,1)} %wout_ref.1), custom_call_target="tpu_custom_call" | custom-call | flops 154618822656 | bytes 150994944 | tf_op jit(solution)/shard_map/mlp/pallas_call | solution.py:569
  583.0 3.9 copy.6

commit v7 on v6

--- a/solution.py
+++ b/solution.py
@@ -380,9 +380,10 @@
         s_copy(k).wait_send()
 
     def phase2(own, sibst):
-        def sib_copy(j):
+        def sib_copy(j, yy):
             w = narrow(j)
-            return remote(sibst.at[:, :, :, w], sibr.at[s2(j), :, :, :, w], sb_s, sb_r.at[s2(j)], sib)
+            src = sibst.at[yy, :, :, w]
+            return remote(src, sibr.at[s2(j), yy, :, :, w], sb_s.at[yy], sb_r.at[s2(j), yy], sib)
 
         def yey_copy(j):
             w = narrow(j)
@@ -438,33 +439,36 @@
             else:
                 pl.when(j + 1 < N - 1)(lambda: fetch(j + 1))
                 pl.when(j + 1 == N - 1)(lambda: fetch(N - 1))
-            when_static(j >= 1, lambda: sib_copy(j - 1).wait_send())
-
-            def part(i, cc):
-                yy, xx = lax.div(i, n_x), lax.rem(i, n_x)
+
+            def part(yy, xx, cc):
                 rows = pl.ds(pl.multiple_of((yy * n_tp + xx * 2 + cc) * R, 16), R)
                 return jnp.dot(h[rows, :], w2b[s2(j), :, W], preferred_element_type=F32)
 
+            for yy in (1, 0):
+                when_static(j >= 1, lambda: sib_copy(j - 1, yy).wait_send())
+
+                @pl.loop(0, n_x)
+                def _(xx):
+                    sibst[yy, xx, :, W] = part(yy, xx, 1 - c)
+
+                sib_copy(j, yy).start()
+
             @pl.loop(0, 2 * n_x)
             def _(i):
-                sibst[lax.div(i, n_x), lax.rem(i, n_x), :, W] = part(i, 1 - c)
-
-            sib_copy(j).start()
-
-            @pl.loop(0, 2 * n_x)
-            def _(i):
-                own[s4(j), lax.div(i, n_x), lax.rem(i, n_x), :, W] = part(i, c)
+                yy, xx = 1 - lax.div(i, n_x), lax.rem(i, n_x)
+                own[s4(j), yy, xx, :, W] = part(yy, xx, c)
 
         def stage1(j):
             W = slice(0, width(j))
-            sib_copy(j).wait_recv()
-
-            @pl.loop(0, 2 * n_x)
-            def _(i):
-                yy, xx = lax.div(i, n_x), lax.rem(i, n_x)
-                own[s4(j), yy, xx, :, W] = own[s4(j), yy, xx, :, W] + sibr[s2(j), yy, xx, :, W]
-
-            send(yey_copy, j)
+            for yy in (1, 0):
+                sib_copy(j, yy).wait_recv()
+
+                @pl.loop(0, n_x)
+                def _(xx):
+                    own[s4(j), yy, xx, :, W] = own[s4(j), yy, xx, :, W] + sibr[s2(j), yy, xx, :, W]
+
+                if yy == 1:
+                    send(yey_copy, j)
             for d in range(2):
                 send(fx_copy, j, d)
 
@@ -534,7 +538,8 @@
                 if j - lag <= N:
                     stage(j - lag)
 
-        sib_copy(N).wait_send()
+        for yy in range(2):
+            sib_copy(N, yy).wait_send()
         for j in (N - 1, N):
             yey_copy(j).wait_send()
             for d in range(2):
@@ -590,7 +595,7 @@
                 dma((2,)), dma((2,)), dma((NB, 4)), dma((6,)), dma((2, 2)), dma((N + 1,)),
                 dma((6,)), dma((6,)), dma((6,)), dma((6,)), dma((6,)), dma((6,)), dma((N,)), dma((N,)),
                 dma((2,)), dma((2,)), dma((2, 2, 2)), dma((2, 2, 2)), dma((2, 2)), dma((2, 2)), dma((2, 8)), dma((2, 8)),
-                dma, dma((2,)), dma((2,)), dma((S,)), dma((2, 2)), dma((S, 2)), dma((2, 2)), dma((S, 2)),
+                dma((2,)), dma((2, 2)), dma((2,)), dma((S,)), dma((2, 2)), dma((S, 2)), dma((2, 2)), dma((S, 2)),
                 dma((2, 2)), dma((S, 2)), dma((2, 2)), dma((S, 2)), dma((2,)), dma((S,)),
             ],
             compiler_params=pltpu.CompilerParams(

time: 588 us -> 586 us (level)
  no operation moved by 1% of the time
where the time goes in v7:
time: 586 us; the launch traced here: 585 us
  Pallas kernels  581 us (99%)
    pallas_call x1, Pallas kernels, local_mlp(): pl.pallas_call(functools.partial(mlp_kernel, n_tp, n_y, N), out_shape=(ja...  581 us

profile of v7, /device:TPU:97, one launch (start us, length us, event | category | flops | bytes accessed | tf_op | source)
XLA Modules:
  0.0 584.6 jit_solution(7068754587355180848)
XLA Ops:
  0.0 580.7 %mlp.1 = (bf16[256,6144]{1,0:T(8,128)(2,1)}, bf16[2,8,256,6144]{3,2,1,0:T(8,128)(2,1)}, bf16[768,6144]{1,0:T(8,128)(2,1)}) custom-call(bf16[256,6144]{1,0:T(8,128)(2,1)} %hid_ref.1, f32[1,6144]{1,0:T(1,128)} %bitcast.1, bf16[1536,3072]{1,0:T(8,128)(2,1)} %win_ref.1, bf16[768,6144]{1,0:T(8,128)(2,1)} %wout_ref.1), custom_call_target="tpu_custom_call" | custom-call | flops 154618822656 | bytes 150994944 | tf_op jit(solution)/shard_map/mlp/pallas_call | solution.py:574
  580.7 3.9 copy.6
